TPU v7x, 256 devices: a whole 4x4x8 slice. The times are simulated.
256 devices in a mesh: gz: 64 (over z, y, core), xy: 4 (over x).
Axes of the slice: x: 4, y: 4, z: 8, core: 2. Of those that a mesh axis runs over, the one named last changes fastest.
Arguments:
- image: float32 [512, 512, 512], P('gz', 'xy'), may hold values from -6 to 6
- offsets: int32 [4, 512, 4, 4], P(None, 'gz', 'xy'), may hold values from -6 to 6
- frac_index: int32 [4, 512, 4, 4], P(None, 'gz', 'xy'), may hold values from 0 to 15
- fractions: float32 [16, 3], replicated, may hold values from 0 to 1
Outputs:
- transported: float32 [512, 512, 512], P('gz', 'xy')
All inputs are finite; a program needn't handle non-finite values.
Results may differ from a plain program's by a relative error of at most 0.0003.
Values sent between devices are 32-bit elements; how exact they have to be, the bound alone decides.
No kernel may reach another device: no remote copies, remote signals or barrier semaphores. Data moves between devices by JAX's collectives and lax.ppermute only.
A program may use at most 128 MiB of HBM per device.

v0:
```python
import jax
import jax.numpy as jnp
from jax import lax
from jax.sharding import PartitionSpec as P


def extended(cells, sides, width):
    for axis, dim in sides:
        count = lax.axis_size(axis)
        head = lax.slice_in_dim(cells, 0, width, axis=dim)
        tail = lax.slice_in_dim(cells, cells.shape[dim] - width, cells.shape[dim], axis=dim)
        cells = jnp.concatenate(
            [
                lax.ppermute(tail, axis, [(i, (i + 1) % count) for i in range(count)]),
                cells,
                lax.ppermute(head, axis, [((i + 1) % count, i) for i in range(count)]),
            ],
            axis=dim,
        )
    return cells


def shifted(x, axis, by):
    devices = lax.axis_size(axis)
    return lax.ppermute(x, axis, [(i, (i + by) % devices) for i in range(devices)])


def cubic_weights(shares):
    return (
        -shares * (shares - 1.0) * (shares - 2.0) / 6.0,
        (shares + 1.0) * (shares - 1.0) * (shares - 2.0) / 2.0,
        -(shares + 1.0) * shares * (shares - 2.0) / 2.0,
        (shares + 1.0) * shares * (shares - 1.0) / 6.0,
    )


def advect(window, shifts_now, index_now, fractions, plane_count, base_row):
    block_size = window.shape[1] - 4
    window_planes = window.shape[0]
    plane_width = window.shape[2]
    block_count = plane_width // block_size
    onehot = (
        index_now[:, :, None] == jnp.arange(fractions.shape[0], dtype=jnp.int32)[None, None, :]
    ).astype(jnp.float32)
    picked = jnp.einsum("pbf,fc->pbc", onehot, fractions, precision=lax.Precision.HIGHEST)
    zweights = cubic_weights(1.0 - picked[:, :, 0])
    xweights = cubic_weights(1.0 - picked[:, :, 1])
    yweights = cubic_weights(1.0 - picked[:, :, 2])
    start_rows = jnp.arange(plane_count, dtype=jnp.int32)[:, None] - shifts_now - 2 + base_row
    levels = jnp.arange(window_planes, dtype=jnp.int32)
    selector = jnp.zeros((plane_count, block_count, window_planes), jnp.float32)
    for node in range(4):
        hits = (levels[None, None, :] == (start_rows + node)[:, :, None]).astype(jnp.float32)
        selector = selector + zweights[node][:, :, None] * hits
    wrapped = jnp.concatenate([window[:, :, -2:], window, window[:, :, :2]], axis=2)
    columns = jnp.stack(
        [
            wrapped[:, :, col * block_size : col * block_size + block_size + 4]
            for col in range(block_count)
        ],
        0,
    )
    merged = jnp.einsum("pbw,bwxy->pbxy", selector, columns, precision=lax.Precision.HIGHEST)
    along_y = jnp.zeros(merged.shape[:3] + (block_size,), jnp.float32)
    for node in range(4):
        along_y = (
            along_y + yweights[node][:, :, None, None] * merged[:, :, :, node : node + block_size]
        )
    along_x = jnp.zeros(merged.shape[:2] + (block_size, block_size), jnp.float32)
    for node in range(4):
        along_x = (
            along_x + xweights[node][:, :, None, None] * along_y[:, :, node : node + block_size, :]
        )
    return along_x.transpose(0, 2, 1, 3).reshape(plane_count, block_size, plane_width)


def local(image, offsets, frac_index, fractions):
    plane_count = image.shape[0]
    reach_hops = -(-8 // plane_count)
    step_count = offsets.shape[0]
    current = image
    for step_index in range(step_count):
        rimmed = extended(current, (("xy", 1),), 2)
        distances = list(range(reach_hops, 0, -1)) + [0] + list(range(-1, -reach_hops - 1, -1))
        pieces = [
            rimmed if distance == 0 else shifted(rimmed, "gz", distance) for distance in distances
        ]
        window = jnp.concatenate(pieces, axis=0)
        current = advect(
            window,
            offsets[step_index, :, 0, :],
            frac_index[step_index, :, 0, :],
            fractions,
            plane_count,
            reach_hops * plane_count,
        )
    return current


def solution(mesh):
    in_specs = (P("gz", "xy", None), P(None, "gz", "xy", None), P(None, "gz", "xy", None), P())
    out_specs = P("gz", "xy", None)
    return jax.shard_map(local, mesh=mesh, in_specs=in_specs, out_specs=out_specs, check_vma=False)
```

profile of v0, /device:TPU:123, one launch (start us, length us, event | category | flops | bytes accessed | tf_op | source)
XLA Modules:
  0.0 239.8 jit_solution(18174599795938720291)
XLA Ops:
  3.9 2.8 %constant_dynamic-update-slice_fusion.1 = f32[8,132,512]{2,0,1:T(8,128)S(1)} fusion(f32[8,132,512]{2,0,1:T(8,128)S(1)} %constant_dynamic-update-slice_fusion.2, f32[8,128,512]{2,1,0:T(8,128)} %param.4), kind=kLoop, calls=%fused_computation.212 | loop fusion | bytes 4194304
  6.7 4.3 %collective-permute-start.2 = (f32[8,132,512]{2,0,1:T(8,128)S(1)}, f32[8,132,512]{2,0,1:T(8,128)S(1)}, u32[]{:S(2)}, u32[]{:S(2)}) collective-permute-start(f32[8,132,512]{2,0,1:T(8,128)S(1)} %constant_dynamic-update-slice_fusion), channel_id=1, source_target_pairs={{0,4},{4,8},{8,12},{12,16},{16,20},{20,24},{24,28},{28,32},{32,36}... | collective-permute-start | bytes 6488072 | tf_op jit(solution)/shard_map/ppermute | solution.py:25
  11.7 23.0 %collective-permute-done.2 = f32[8,132,512]{2,0,1:T(8,128)S(1)} collective-permute-done((f32[8,132,512]{2,0,1:T(8,128)S(1)}, f32[8,132,512]{2,0,1:T(8,128)S(1)}, u32[]{:S(2)}, u32[]{:S(2)}) %collective-permute-start.2) | collective-permute-done | bytes 2162720 | tf_op jit(solution)/shard_map/ppermute | solution.py:25
  34.7 6.0 %collective-permute-done.3 = f32[8,132,512]{2,0,1:T(8,128)S(1)} collective-permute-done((f32[8,132,512]{2,0,1:T(8,128)S(1)}, f32[8,132,512]{2,0,1:T(8,128)S(1)}, u32[]{:S(2)}, u32[]{:S(2)}) %collective-permute-start.3) | collective-permute-done | bytes 2162720 | tf_op jit(solution)/shard_map/ppermute | solution.py:25
  42.3 7.7 %slice_bitcast_fusion.7 = (f32[1,24,132,132]{3,1,2,0:T(8,128)S(1)}, f32[1,24,132,132]{3,1,2,0:T(8,128)}, f32[1,24,132,132]{3,1,2,0:T(8,128)}, f32[1,24,132,132]{3,1,2,0:T(8,128)}) fusion(f32[24,132,512]{2,0,1:T(8,128)S(1)} %pad_maximum_fusion, f32[24,132,2]{2,0,1:T(8,128)S(1)} %get-tuple-element.26, f32[8,132,512]{2,0,1:T(8,128)S(1)} %collective-permute-done.3, ...), kind=kLoop, calls=%fused_computation.83 | loop fusion | flops 2509056 | bytes 16574976 | tf_op jit(solution)/shard_map/stack | solution.py:56
  50.0 9.6 %fusion.49 = f32[8,4,132,132]{3,0,2,1:T(8,128)S(1)} fusion(f32[1,24,132,132]{3,1,2,0:T(8,128)} %get-tuple-element.137, f32[1,24,132,132]{3,1,2,0:T(8,128)} %get-tuple-element.28, f32[1,24,132,132]{3,1,2,0:T(8,128)S(1)} %get-tuple-element.27, f32[1,24,132,132]{3,1,2,0:T(8,128)} %get-tuple-element.138, f32[8,4]{0,1:T(4,128)S(1)} %bitcast.215, ...), kind=kOutput, calls=%fused_computation.91 | convolution fusion | flops 165606144 | bytes 8922112 | tf_op jit(solution)/shard_map/pbw,bwxy->pbxy/dot_general | solution.py:63
  63.8 2.2 copy.12
  72.3 23.3 %collective-permute-done.6 = f32[8,132,512]{2,0,1:T(8,128)S(1)} collective-permute-done((f32[8,132,512]{2,0,1:T(8,128)S(1)}, f32[8,132,512]{2,0,1:T(8,128)S(1)}, u32[]{:S(2)}, u32[]{:S(2)}) %collective-permute-start.6) | collective-permute-done | bytes 2162720 | tf_op jit(solution)/shard_map/ppermute | solution.py:25
  95.6 5.8 %collective-permute-done.7 = f32[8,132,512]{2,0,1:T(8,128)S(1)} collective-permute-done((f32[8,132,512]{2,0,1:T(8,128)S(1)}, f32[8,132,512]{2,0,1:T(8,128)S(1)}, u32[]{:S(2)}, u32[]{:S(2)}) %collective-permute-start.7) | collective-permute-done | bytes 2162720 | tf_op jit(solution)/shard_map/ppermute | solution.py:25
  104.7 5.3 %fusion.37 = (f32[1,24,132,132]{3,1,2,0:T(8,128)S(1)}, f32[1,24,132,132]{3,1,2,0:T(8,128)S(1)}) fusion(f32[24,132,2]{2,0,1:T(8,128)S(1)} %get-tuple-element.19, f32[8,132,512]{2,0,1:T(8,128)S(1)} %collective-permute-done.7, f32[8,132,512]{2,0,1:T(8,128)S(1)} %collective-permute-done.6, f32[8,2,512]{2,0,1:T(8,128)S(1)} %collective-permute-done.5, ...), kind=kLoop, calls=%fused_computation.73 | loop fusion | flops 4181760 | bytes 9884160 | tf_op jit(solution)/shard_map/stack | solution.py:56
  110.1 7.0 %fusion.46 = f32[8,4,132,132]{3,0,2,1:T(8,128)S(1)} fusion(f32[1,24,132,132]{3,1,2,0:T(8,128)S(1)} %get-tuple-element.18, f32[1,24,132,132]{3,1,2,0:T(8,128)S(1)} %get-tuple-element.22, f32[1,24,132,132]{3,1,2,0:T(8,128)S(1)} %get-tuple-element.21, f32[1,24,132,132]{3,1,2,0:T(8,128)S(1)} %get-tuple-element.17, f32[8,4]{0,1:T(4,128)S(1)} %bitcast.223, ...), kind=kOutput, calls=%fused_computation.90 | convolution fusion | flops 165606144 | bytes 8922112 | tf_op jit(solution)/shard_map/pbw,bwxy->pbxy/dot_general | solution.py:63
  121.2 2.2 copy.16
  126.6 2.2 collective-permute-done.9
  130.3 23.3 %collective-permute-done.10 = f32[8,132,512]{2,0,1:T(8,128)S(1)} collective-permute-done((f32[8,132,512]{2,0,1:T(8,128)S(1)}, f32[8,132,512]{2,0,1:T(8,128)S(1)}, u32[]{:S(2)}, u32[]{:S(2)}) %collective-permute-start.10) | collective-permute-done | bytes 2162720 | tf_op jit(solution)/shard_map/ppermute | solution.py:25
  153.6 5.8 %collective-permute-done.11 = f32[8,132,512]{2,0,1:T(8,128)S(1)} collective-permute-done((f32[8,132,512]{2,0,1:T(8,128)S(1)}, f32[8,132,512]{2,0,1:T(8,128)S(1)}, u32[]{:S(2)}, u32[]{:S(2)}) %collective-permute-start.11) | collective-permute-done | bytes 2162720 | tf_op jit(solution)/shard_map/ppermute | solution.py:25
  162.7 4.8 %fusion.35 = (f32[1,24,132,132]{3,1,2,0:T(8,128)S(1)}, f32[1,24,132,132]{3,1,2,0:T(8,128)S(1)}) fusion(f32[24,132,2]{2,0,1:T(8,128)S(1)} %get-tuple-element.13, f32[8,132,512]{2,0,1:T(8,128)S(1)} %collective-permute-done.11, f32[8,132,512]{2,0,1:T(8,128)S(1)} %collective-permute-done.10, f32[8,2,512]{2,0,1:T(8,128)S(1)} %collective-permute-done.9, ...), kind=kLoop, calls=%fused_computation.59 | loop fusion | flops 4181760 | bytes 9884160 | tf_op jit(solution)/shard_map/stack | solution.py:56
  167.5 7.0 %fusion.43 = f32[8,4,132,132]{3,0,2,1:T(8,128)S(1)} fusion(f32[1,24,132,132]{3,1,2,0:T(8,128)S(1)} %get-tuple-element.12, f32[1,24,132,132]{3,1,2,0:T(8,128)S(1)} %get-tuple-element.16, f32[1,24,132,132]{3,1,2,0:T(8,128)S(1)} %get-tuple-element.15, f32[1,24,132,132]{3,1,2,0:T(8,128)S(1)} %get-tuple-element.11, f32[8,4]{0,1:T(4,128)S(1)} %bitcast.227, ...), kind=kOutput, calls=%fused_computation.89 | convolution fusion | flops 165606144 | bytes 8922112 | tf_op jit(solution)/shard_map/pbw,bwxy->pbxy/dot_general | solution.py:63
  178.6 2.2 copy.20
  183.7 2.2 collective-permute-done.13
  187.7 23.3 %collective-permute-done.14 = f32[8,132,512]{2,0,1:T(8,128)S(1)} collective-permute-done((f32[8,132,512]{2,0,1:T(8,128)S(1)}, f32[8,132,512]{2,0,1:T(8,128)S(1)}, u32[]{:S(2)}, u32[]{:S(2)}) %collective-permute-start.14) | collective-permute-done | bytes 2162720 | tf_op jit(solution)/shard_map/ppermute | solution.py:25
  211.1 5.8 %collective-permute-done.15 = f32[8,132,512]{2,0,1:T(8,128)S(1)} collective-permute-done((f32[8,132,512]{2,0,1:T(8,128)S(1)}, f32[8,132,512]{2,0,1:T(8,128)S(1)}, u32[]{:S(2)}, u32[]{:S(2)}) %collective-permute-start.15) | collective-permute-done | bytes 2162720 | tf_op jit(solution)/shard_map/ppermute | solution.py:25
  220.1 5.2 %fusion.33 = (f32[1,24,132,132]{3,1,2,0:T(8,128)S(1)}, f32[1,24,132,132]{3,1,2,0:T(8,128)S(1)}) fusion(f32[24,132,2]{2,0,1:T(8,128)S(1)} %get-tuple-element.7, f32[8,132,512]{2,0,1:T(8,128)S(1)} %collective-permute-done.15, f32[8,132,512]{2,0,1:T(8,128)S(1)} %collective-permute-done.14, f32[8,2,512]{2,0,1:T(8,128)S(1)} %collective-permute-done.13, ...), kind=kLoop, calls=%fused_computation.45 | loop fusion | flops 4181760 | bytes 9884160 | tf_op jit(solution)/shard_map/stack | solution.py:56
  225.3 7.0 %fusion.40 = f32[8,4,132,132]{3,0,2,1:T(8,128)S(1)} fusion(f32[1,24,132,132]{3,1,2,0:T(8,128)S(1)} %get-tuple-element.6, f32[1,24,132,132]{3,1,2,0:T(8,128)S(1)} %get-tuple-element.10, f32[1,24,132,132]{3,1,2,0:T(8,128)S(1)} %get-tuple-element.9, f32[1,24,132,132]{3,1,2,0:T(8,128)S(1)} %get-tuple-element.5, f32[8,4]{0,1:T(4,128)S(1)} %bitcast.219, ...), kind=kOutput, calls=%fused_computation.88 | convolution fusion | flops 165606144 | bytes 8922112 | tf_op jit(solution)/shard_map/pbw,bwxy->pbxy/dot_general | solution.py:63
  235.9 1.9 copy.23
  (79 shorter events, 49.0 us)
Async XLA Ops:
  0.0 11.3 %copy-start = (f32[16,3]{0,1:T(4,128)S(1)}, f32[16,3]{0,1:T(4,128)}, u32[]{:S(2)}) copy-start(f32[16,3]{0,1:T(4,128)} %param.7) | copy-start | bytes 580
  1.0 2.8 %collective-permute-start = (f32[8,2,512]{2,0,1:T(8,128)S(1)}, f32[8,2,512]{2,0,1:T(8,128)S(1)}, u32[]{:S(2)}, u32[]{:S(2)}) collective-permute-start(f32[8,2,512]{2,0,1:T(8,128)S(1)} %copy.30), channel_id=1, source_target_pairs={{0,1},{1,2},{2,3},{3,0},{4,5},{5,6},{6,7},{7,4},{8,9},{9,10},{10,1... | collective-permute-start | bytes 98312 | tf_op jit(solution)/shard_map/ppermute | solution.py:14
  2.3 8.9 %copy-start.2 = (s32[4,8,1,4]{1,3,2,0:T(4,128)S(1)}, s32[4,8,1,4]{1,3,2,0:T(4,128)}, u32[]{:S(2)}) copy-start(s32[4,8,1,4]{1,3,2,0:T(4,128)} %param.6) | copy-start | bytes 1540
  2.3 4.4 %collective-permute-start.1 = (f32[8,2,512]{2,0,1:T(8,128)S(1)}, f32[8,2,512]{2,0,1:T(8,128)S(1)}, u32[]{:S(2)}, u32[]{:S(2)}) collective-permute-start(f32[8,2,512]{2,0,1:T(8,128)S(1)} %copy.31), channel_id=1, source_target_pairs={{1,0},{2,1},{3,2},{0,3},{5,4},{6,5},{7,6},{4,7},{9,8},{10,9},{11,1... | collective-permute-start | bytes 98312 | tf_op jit(solution)/shard_map/ppermute | solution.py:16
  3.9 7.8 %copy-start.1 = (s32[4,8,1,4]{1,3,2,0:T(4,128)S(1)}, s32[4,8,1,4]{1,3,2,0:T(4,128)}, u32[]{:S(2)}) copy-start(s32[4,8,1,4]{1,3,2,0:T(4,128)} %param.5) | copy-start | bytes 1540
  6.7 28.0 %collective-permute-start.2 = (f32[8,132,512]{2,0,1:T(8,128)S(1)}, f32[8,132,512]{2,0,1:T(8,128)S(1)}, u32[]{:S(2)}, u32[]{:S(2)}) collective-permute-start(f32[8,132,512]{2,0,1:T(8,128)S(1)} %constant_dynamic-update-slice_fusion), channel_id=1, source_target_pairs={{0,4},{4,8},{8,12},{12,16},{16,20},{20,24},{24,28},{28,32},{32,36}... | collective-permute-start | bytes 6488072 | tf_op jit(solution)/shard_map/ppermute | solution.py:25
  11.0 29.7 %collective-permute-start.3 = (f32[8,132,512]{2,0,1:T(8,128)S(1)}, f32[8,132,512]{2,0,1:T(8,128)S(1)}, u32[]{:S(2)}, u32[]{:S(2)}) collective-permute-start(f32[8,132,512]{2,0,1:T(8,128)S(1)} %constant_dynamic-update-slice_fusion), channel_id=1, source_target_pairs={{0,252},{4,0},{8,4},{12,8},{16,12},{20,16},{24,20},{28,24},{32,28}... | collective-permute-start | bytes 6488072 | tf_op jit(solution)/shard_map/ppermute | solution.py:25
  66.0 3.1 %collective-permute-start.4 = (f32[8,2,512]{2,0,1:T(8,128)S(1)}, f32[8,2,512]{2,0,1:T(8,128)S(1)}, u32[]{:S(2)}, u32[]{:S(2)}) collective-permute-start(f32[8,2,512]{2,0,1:T(8,128)S(1)} %get-tuple-element.33), channel_id=1, source_target_pairs={{0,1},{1,2},{2,3},{3,0},{4,5},{5,6},{6,7},{7,4},{8,9},{9,10},{10,1... | collective-permute-start | bytes 98312 | tf_op jit(solution)/shard_map/ppermute | solution.py:14
  67.3 3.3 %collective-permute-start.5 = (f32[8,2,512]{2,0,1:T(8,128)S(1)}, f32[8,2,512]{2,0,1:T(8,128)S(1)}, u32[]{:S(2)}, u32[]{:S(2)}) collective-permute-start(f32[8,2,512]{2,0,1:T(8,128)S(1)} %get-tuple-element.34), channel_id=1, source_target_pairs={{1,0},{2,1},{3,2},{0,3},{5,4},{6,5},{7,6},{4,7},{9,8},{10,9},{11,1... | collective-permute-start | bytes 98312 | tf_op jit(solution)/shard_map/ppermute | solution.py:16
  70.8 24.8 %collective-permute-start.6 = (f32[8,132,512]{2,0,1:T(8,128)S(1)}, f32[8,132,512]{2,0,1:T(8,128)S(1)}, u32[]{:S(2)}, u32[]{:S(2)}) collective-permute-start(f32[8,132,512]{2,0,1:T(8,128)S(1)} %pad_maximum_fusion.40), channel_id=1, source_target_pairs={{0,4},{4,8},{8,12},{12,16},{16,20},{20,24},{24,28},{28,32},{32,36}... | collective-permute-start | bytes 6488072 | tf_op jit(solution)/shard_map/ppermute | solution.py:25
  72.0 29.5 %collective-permute-start.7 = (f32[8,132,512]{2,0,1:T(8,128)S(1)}, f32[8,132,512]{2,0,1:T(8,128)S(1)}, u32[]{:S(2)}, u32[]{:S(2)}) collective-permute-start(f32[8,132,512]{2,0,1:T(8,128)S(1)} %pad_maximum_fusion.40), channel_id=1, source_target_pairs={{0,252},{4,0},{8,4},{12,8},{16,12},{20,16},{24,20},{28,24},{32,28}... | collective-permute-start | bytes 6488072 | tf_op jit(solution)/shard_map/ppermute | solution.py:25
  123.5 3.1 %collective-permute-start.8 = (f32[8,2,512]{2,0,1:T(8,128)S(1)}, f32[8,2,512]{2,0,1:T(8,128)S(1)}, u32[]{:S(2)}, u32[]{:S(2)}) collective-permute-start(f32[8,2,512]{2,0,1:T(8,128)S(1)} %get-tuple-element.31), channel_id=1, source_target_pairs={{0,1},{1,2},{2,3},{3,0},{4,5},{5,6},{6,7},{7,4},{8,9},{9,10},{10,1... | collective-permute-start | bytes 98312 | tf_op jit(solution)/shard_map/ppermute | solution.py:14
  124.5 4.4 %collective-permute-start.9 = (f32[8,2,512]{2,0,1:T(8,128)S(1)}, f32[8,2,512]{2,0,1:T(8,128)S(1)}, u32[]{:S(2)}, u32[]{:S(2)}) collective-permute-start(f32[8,2,512]{2,0,1:T(8,128)S(1)} %get-tuple-element.32), channel_id=1, source_target_pairs={{1,0},{2,1},{3,2},{0,3},{5,4},{6,5},{7,6},{4,7},{9,8},{10,9},{11,1... | collective-permute-start | bytes 98312 | tf_op jit(solution)/shard_map/ppermute | solution.py:16
  129.0 24.6 %collective-permute-start.10 = (f32[8,132,512]{2,0,1:T(8,128)S(1)}, f32[8,132,512]{2,0,1:T(8,128)S(1)}, u32[]{:S(2)}, u32[]{:S(2)}) collective-permute-start(f32[8,132,512]{2,0,1:T(8,128)S(1)} %pad_maximum_fusion.41), channel_id=1, source_target_pairs={{0,4},{4,8},{8,12},{12,16},{16,20},{20,24},{24,28},{28,32},{32,36}... | collective-permute-start | bytes 6488072 | tf_op jit(solution)/shard_map/ppermute | solution.py:25
  130.0 29.5 %collective-permute-start.11 = (f32[8,132,512]{2,0,1:T(8,128)S(1)}, f32[8,132,512]{2,0,1:T(8,128)S(1)}, u32[]{:S(2)}, u32[]{:S(2)}) collective-permute-start(f32[8,132,512]{2,0,1:T(8,128)S(1)} %pad_maximum_fusion.41), channel_id=1, source_target_pairs={{0,252},{4,0},{8,4},{12,8},{16,12},{20,16},{24,20},{28,24},{32,28}... | collective-permute-start | bytes 6488072 | tf_op jit(solution)/shard_map/ppermute | solution.py:25
  180.9 2.8 %collective-permute-start.12 = (f32[8,2,512]{2,0,1:T(8,128)S(1)}, f32[8,2,512]{2,0,1:T(8,128)S(1)}, u32[]{:S(2)}, u32[]{:S(2)}) collective-permute-start(f32[8,2,512]{2,0,1:T(8,128)S(1)} %get-tuple-element.29), channel_id=1, source_target_pairs={{0,1},{1,2},{2,3},{3,0},{4,5},{5,6},{6,7},{7,4},{8,9},{9,10},{10,1... | collective-permute-start | bytes 98312 | tf_op jit(solution)/shard_map/ppermute | solution.py:14
  182.7 3.2 %collective-permute-start.13 = (f32[8,2,512]{2,0,1:T(8,128)S(1)}, f32[8,2,512]{2,0,1:T(8,128)S(1)}, u32[]{:S(2)}, u32[]{:S(2)}) collective-permute-start(f32[8,2,512]{2,0,1:T(8,128)S(1)} %get-tuple-element.30), channel_id=1, source_target_pairs={{1,0},{2,1},{3,2},{0,3},{5,4},{6,5},{7,6},{4,7},{9,8},{10,9},{11,1... | collective-permute-start | bytes 98312 | tf_op jit(solution)/shard_map/ppermute | solution.py:16
  186.2 24.9 %collective-permute-start.14 = (f32[8,132,512]{2,0,1:T(8,128)S(1)}, f32[8,132,512]{2,0,1:T(8,128)S(1)}, u32[]{:S(2)}, u32[]{:S(2)}) collective-permute-start(f32[8,132,512]{2,0,1:T(8,128)S(1)} %pad_maximum_fusion.42), channel_id=1, source_target_pairs={{0,4},{4,8},{8,12},{12,16},{16,20},{20,24},{24,28},{28,32},{32,36}... | collective-permute-start | bytes 6488072 | tf_op jit(solution)/shard_map/ppermute | solution.py:25
  187.4 29.5 %collective-permute-start.15 = (f32[8,132,512]{2,0,1:T(8,128)S(1)}, f32[8,132,512]{2,0,1:T(8,128)S(1)}, u32[]{:S(2)}, u32[]{:S(2)}) collective-permute-start(f32[8,132,512]{2,0,1:T(8,128)S(1)} %pad_maximum_fusion.42), channel_id=1, source_target_pairs={{0,252},{4,0},{8,4},{12,8},{16,12},{20,16},{24,20},{28,24},{32,28}... | collective-permute-start | bytes 6488072 | tf_op jit(solution)/shard_map/ppermute | solution.py:25
where the time goes:
time: 244 us; the launch traced here: 240 us
  waiting for transfers between devices  127 us (52%)
  other arithmetic  38 us (16%)
  matrix products  31.8 us (13%)
  local copies, waits for them, and re-layouts  27.4 us (11%)
  starting transfers between devices  15.1 us (6%)
    ppermute x8, waiting for transfers between devices, shifted(): lax.ppermute(x, axis, [(i, (i + by) % devices) for i in range(devices)])  116 us
    dot_general x4, matrix products, advect(): jnp.einsum('pbw,bwxy->pbxy', selector, columns, precision=lax.Precision.H...  30.7 us
    another operation x4, other arithmetic, advect(): jnp.stack([wrapped[:, :, col * block_size:col * block_size + block_size +...  22.9 us
    reshape x4, local copies, waits for them, and re-layouts, advect(): along_x.transpose(0, 2, 1, 3).reshape(plane_count, block_size, plane_width)  8.55 us
    ppermute x8, starting transfers between devices, shifted(): lax.ppermute(x, axis, [(i, (i + by) % devices) for i in range(devices)])  7.81 us
    transpose x4, local copies, waits for them, and re-layouts, advect(): along_x.transpose(0, 2, 1, 3).reshape(plane_count, block_size, plane_width)  7.4 us
    add x4, other arithmetic, advect(): along_y + yweights[node][:, :, None, None] * merged[:, :, :, node:node +...  7.01 us
    ppermute x4, waiting for transfers between devices, extended(): lax.ppermute(head, axis, [((i + 1) % count, i) for i in range(count)])  5.94 us
  transfers between devices with their start and end apart: 16, of which 15 were waited for; matrix products, arithmetic and copies ran while one was open for 2% of the time, Pallas kernels for 0%

commit v1 on v0

v1 whole, which is shorter than its diff:
```python
import jax
import jax.numpy as jnp
from jax import lax
from jax.experimental import pallas as pl
from jax.experimental.pallas import tpu as pltpu
from jax.sharding import PartitionSpec as P

REACH = 8
LANES = 128


def cubic_weights(shares):
    return (
        -shares * (shares - 1.0) * (shares - 2.0) / 6.0,
        (shares + 1.0) * (shares - 1.0) * (shares - 2.0) / 2.0,
        -(shares + 1.0) * shares * (shares - 2.0) / 2.0,
        (shares + 1.0) * shares * (shares - 1.0) / 6.0,
    )


def weight_table(fractions):
    parts = [jnp.stack(cubic_weights(1.0 - fractions[:, axis]), axis=1) for axis in range(3)]
    return jnp.concatenate(parts, axis=1).reshape(-1)


def advect_body(planes, rows, per_step, off_ref, idx_ref, tab_ref, up, own, down, rim_up, rim_own, rim_down, out_ref, win, line, sems):
    blocks = win.shape[2] // LANES

    @pl.when(pl.program_id(0) == 0)
    def _():
        pieces = [
            (up, 0, REACH, 8, rows),
            (own, REACH, planes, 8, rows),
            (down, REACH + planes, REACH, 8, rows),
            (rim_up, 0, REACH, 0, 8),
            (rim_own, REACH, planes, 0, 8),
            (rim_down, REACH + planes, REACH, 0, 8),
        ]
        copies = [
            pltpu.make_async_copy(src, win.at[pl.ds(first, count), pl.ds(row, height), :], sems.at[i])
            for i, (src, first, count, row, height) in enumerate(pieces)
        ]
        for copy in copies:
            copy.start()
        for copy in copies:
            copy.wait()

    lane = lax.broadcasted_iota(jnp.int32, (8, LANES), 1)
    from_right = lane < 64
    last_two = lane >= LANES - 2
    last_one = lane >= LANES - 1
    first_one = lane == 0
    tiles = rows // 8 + 1

    def plane(local, carry):
        k = pl.program_id(0) * per_step + local
        for b in range(blocks):
            left = ((b - 1) % blocks) * LANES
            right = ((b + 1) % blocks) * LANES
            base = k - off_ref[k * blocks + b] + (REACH - 2)
            entry = idx_ref[k * blocks + b] * 12
            cz = [tab_ref[entry + n] for n in range(4)]
            cx = [tab_ref[entry + 4 + n] for n in range(4)]
            cy = [tab_ref[entry + 8 + n] for n in range(4)]
            for t in range(tiles):
                here = pl.ds(t * 8, 8)
                mid = None
                edge = None
                for n in range(4):
                    m = cz[n] * win[base + n, here, pl.ds(b * LANES, LANES)]
                    e = cz[n] * jnp.where(
                        from_right,
                        win[base + n, here, pl.ds(right, LANES)],
                        win[base + n, here, pl.ds(left, LANES)],
                    )
                    mid = m if mid is None else mid + m
                    edge = e if edge is None else edge + e
                y = cy[2] * mid
                y = y + cy[0] * pltpu.roll(jnp.where(last_two, edge, mid), 2, 1)
                y = y + cy[1] * pltpu.roll(jnp.where(last_one, edge, mid), 1, 1)
                y = y + cy[3] * pltpu.roll(jnp.where(first_one, edge, mid), LANES - 1, 1)
                line[b, here, :] = y
                if t == 0:
                    line[b, pl.ds(tiles * 8, 8), :] = y
            for t in range(1, tiles):
                acc = cx[0] * line[b, pl.ds(t * 8 - 2, 8), :]
                for n in range(1, 4):
                    acc = acc + cx[n] * line[b, pl.ds(t * 8 - 2 + n, 8), :]
                out_ref[local, pl.ds((t - 1) * 8, 8), pl.ds(b * LANES, LANES)] = acc
        return carry

    lax.fori_loop(0, per_step, plane, 0)


def advect(up, own, down, rim_up, rim_own, rim_down, offsets, index, table, per_step):
    planes, rows, width = own.shape
    blocks = width // LANES

    def body(*refs):
        advect_body(planes, rows, per_step, *refs)

    anywhere = pl.BlockSpec(memory_space=pl.ANY)
    return pl.pallas_call(
        body,
        out_shape=jax.ShapeDtypeStruct(own.shape, jnp.float32),
        grid_spec=pltpu.PrefetchScalarGridSpec(
            num_scalar_prefetch=3,
            grid=(planes // per_step,),
            in_specs=[anywhere] * 6,
            out_specs=pl.BlockSpec((per_step, rows, width), lambda i, *_: (i, 0, 0)),
            scratch_shapes=[
                pltpu.VMEM((planes + 2 * REACH, rows + 8, width), jnp.float32),
                pltpu.VMEM((blocks, rows + 16, LANES), jnp.float32),
                pltpu.SemaphoreType.DMA((6,)),
            ],
        ),
        name="advect",
    )(offsets, index, table, up, own, down, rim_up, rim_own, rim_down)


def shifted(x, axis, by):
    devices = lax.axis_size(axis)
    return lax.ppermute(x, axis, [(i, (i + by) % devices) for i in range(devices)])


def local(image, offsets, frac_index, fractions):
    planes, rows, width = image.shape
    table = weight_table(fractions)
    current = image
    for step in range(offsets.shape[0]):
        up = shifted(current, "gz", 1)
        down = shifted(current, "gz", -1)
        above = shifted(current[:, rows - 2 :], "xy", 1)
        below = shifted(current[:, :2], "xy", -1)
        rim = jnp.concatenate([below, jnp.zeros((planes, 4, width), jnp.float32), above], axis=1)
        rim_up = shifted(rim, "gz", 1)
        rim_down = shifted(rim, "gz", -1)
        current = advect(
            up, current, down, rim_up, rim, rim_down,
            offsets[step].reshape(-1), frac_index[step].reshape(-1), table, 1,
        )
    return current


def solution(mesh):
    in_specs = (P("gz", "xy", None), P(None, "gz", "xy", None), P(None, "gz", "xy", None), P())
    out_specs = P("gz", "xy", None)
    return jax.shard_map(local, mesh=mesh, in_specs=in_specs, out_specs=out_specs, check_vma=False)
```

time: 244 us -> 170 us (0.70)
  the two profiles are of different devices: /device:TPU:123 before, /device:TPU:6 now
where the time goes in v1:
time: 170 us
  waiting for transfers between devices  78.4 us (46%)
  starting transfers between devices  38.3 us (23%)
  Pallas kernels  34.7 us (20%)
  local copies, waits for them, and re-layouts  17.4 us (10%)
    ppermute x24, waiting for transfers between devices, shifted(): lax.ppermute(x, axis, [(i, (i + by) % devices) for i in range(devices)])  78.4 us
    ppermute x24, starting transfers between devices, shifted(): lax.ppermute(x, axis, [(i, (i + by) % devices) for i in range(devices)])  38.3 us
    pallas_call x4, Pallas kernels, advect(): pl.pallas_call(body, out_shape=jax.ShapeDtypeStruct(own.shape, jnp.float3...  34.7 us
    unnamed x32, local copies, waits for them, and re-layouts  5.4 us
    slice x4, local copies, waits for them, and re-layouts, local(): below = shifted(current[:, :2], 'xy', -1)  3.98 us
  transfers between devices with their start and end apart: 24, of which 11 were waited for; matrix products, arithmetic and copies ran while one was open for 8% of the time, Pallas kernels for 0%

profile of v1, /device:TPU:6, one launch (start us, length us, event | category | flops | bytes accessed | tf_op | source)
XLA Modules:
  0.0 170.2 jit_solution(720600343517905608)
XLA Ops:
  0.0 7.7 %collective-permute-start.1 = (f32[8,128,512]{2,1,0:T(8,128)}, f32[8,128,512]{2,1,0:T(8,128)S(1)}, u32[]{:S(2)}, u32[]{:S(2)}) collective-permute-start(f32[8,128,512]{2,1,0:T(8,128)} %refs_4_.1), channel_id=1, source_target_pairs={{0,252},{4,0},{8,4},{12,8},{16,12},{20,16},{24,20},{28,24},{32,28}... | collective-permute-start | bytes 6291464 | tf_op jit(solution)/shard_map/ppermute | solution.py:123
  9.7 2.4 %collective-permute-start.3 = (f32[8,2,512]{2,1,0:T(2,128)S(1)}, f32[8,2,512]{2,1,0:T(2,128)S(1)}, u32[]{:S(2)}, u32[]{:S(2)}) collective-permute-start(f32[8,2,512]{2,1,0:T(2,128)S(1)} %get-tuple-element.12), channel_id=1, source_target_pairs={{0,1},{1,2},{2,3},{3,0},{4,5},{5,6},{6,7},{7,4},{8,9},{9,10},{10,1... | collective-permute-start | bytes 98312 | tf_op jit(solution)/shard_map/ppermute | solution.py:123
  15.3 4.6 %collective-permute-start.5 = (f32[8,8,512]{2,1,0:T(8,128)S(1)}, f32[8,8,512]{2,1,0:T(8,128)S(1)}, u32[]{:S(2)}, u32[]{:S(2)}) collective-permute-start(f32[8,8,512]{2,1,0:T(8,128)S(1)} %pad_maximum_fusion.refs_7_), channel_id=1, source_target_pairs={{0,252},{4,0},{8,4},{12,8},{16,12},{20,16},{24,20},{28,24},{32,28}... | collective-permute-start | bytes 393224 | tf_op jit(solution)/shard_map/ppermute | solution.py:123
  21.3 11.6 %collective-permute-done.5.refs_8_ = f32[8,8,512]{2,1,0:T(8,128)S(1)} collective-permute-done((f32[8,8,512]{2,1,0:T(8,128)S(1)}, f32[8,8,512]{2,1,0:T(8,128)S(1)}, u32[]{:S(2)}, u32[]{:S(2)}) %collective-permute-start.5) | collective-permute-done | bytes 131104 | tf_op jit(solution)/shard_map/ppermute | solution.py:123
  32.9 5.2 %collective-permute-done.4.refs_6_ = f32[8,8,512]{2,1,0:T(8,128)S(1)} collective-permute-done((f32[8,8,512]{2,1,0:T(8,128)S(1)}, f32[8,8,512]{2,1,0:T(8,128)S(1)}, u32[]{:S(2)}, u32[]{:S(2)}) %collective-permute-start.4) | collective-permute-done | bytes 131104 | tf_op jit(solution)/shard_map/ppermute | solution.py:123
  39.5 8.7 %advect.4.refs_4_ = f32[8,128,512]{2,1,0:T(8,128)} custom-call(s32[32]{0:T(128)} %reshape_squeeze.30.refs_0_, s32[32]{0:T(128)} %reshape_squeeze.31.refs_1_, f32[192]{0:T(256)} %reshape.3.refs_2_, f32[8,128,512]{2,1,0:T(8,128)} %collective-permute-done.refs_3_, f32[8,128,512]{2,1,0:T(8,128)} %refs_4_.1, f32[8,128,512]{2,1,0:T(8,128)} %copy-done, ...), custom_call_target="tpu_custom_call" | custom-call | tf_op jit(solution)/shard_map/advect/pallas_call | solution.py:103
  50.7 2.4 %collective-permute-start.9 = (f32[8,2,512]{2,1,0:T(2,128)S(1)}, f32[8,2,512]{2,1,0:T(2,128)S(1)}, u32[]{:S(2)}, u32[]{:S(2)}) collective-permute-start(f32[8,2,512]{2,1,0:T(2,128)S(1)} %get-tuple-element.10), channel_id=1, source_target_pairs={{0,1},{1,2},{2,3},{3,0},{4,5},{5,6},{6,7},{7,4},{8,9},{9,10},{10,1... | collective-permute-start | bytes 98312 | tf_op jit(solution)/shard_map/ppermute | solution.py:123
  53.1 1.9 %collective-permute-done.8 = f32[8,2,512]{2,1,0:T(2,128)S(1)} collective-permute-done((f32[8,2,512]{2,1,0:T(2,128)S(1)}, f32[8,2,512]{2,1,0:T(2,128)S(1)}, u32[]{:S(2)}, u32[]{:S(2)}) %collective-permute-start.8) | collective-permute-done | bytes 32800 | tf_op jit(solution)/shard_map/ppermute | solution.py:123
  55.1 3.6 %collective-permute-start.11 = (f32[8,8,512]{2,1,0:T(8,128)S(1)}, f32[8,8,512]{2,1,0:T(8,128)S(1)}, u32[]{:S(2)}, u32[]{:S(2)}) collective-permute-start(f32[8,8,512]{2,1,0:T(8,128)S(1)} %pad_maximum_fusion.1.refs_7_), channel_id=1, source_target_pairs={{0,252},{4,0},{8,4},{12,8},{16,12},{20,16},{24,20},{28,24},{32,28}... | collective-permute-start | bytes 393224 | tf_op jit(solution)/shard_map/ppermute | solution.py:123
  60.1 13.4 %collective-permute-done.11.refs_8_ = f32[8,8,512]{2,1,0:T(8,128)S(1)} collective-permute-done((f32[8,8,512]{2,1,0:T(8,128)S(1)}, f32[8,8,512]{2,1,0:T(8,128)S(1)}, u32[]{:S(2)}, u32[]{:S(2)}) %collective-permute-start.11) | collective-permute-done | bytes 131104 | tf_op jit(solution)/shard_map/ppermute | solution.py:123
  73.5 5.3 %collective-permute-done.10.refs_6_ = f32[8,8,512]{2,1,0:T(8,128)S(1)} collective-permute-done((f32[8,8,512]{2,1,0:T(8,128)S(1)}, f32[8,8,512]{2,1,0:T(8,128)S(1)}, u32[]{:S(2)}, u32[]{:S(2)}) %collective-permute-start.10) | collective-permute-done | bytes 131104 | tf_op jit(solution)/shard_map/ppermute | solution.py:123
  80.1 8.7 %advect.5.refs_4_ = f32[8,128,512]{2,1,0:T(8,128)} custom-call(s32[32]{0:T(128)} %reshape_squeeze.28.refs_0_, s32[32]{0:T(128)} %reshape_squeeze.29.refs_1_, f32[192]{0:T(256)} %reshape.3.refs_2_, f32[8,128,512]{2,1,0:T(8,128)} %collective-permute-done.6.refs_3_, f32[8,128,512]{2,1,0:T(8,128)} %advect.4.refs_4_, f32[8,128,512]{2,1,0:T(8,128)} %copy-done.2, ...), custom_call_target="tpu_custom_call" | custom-call | tf_op jit(solution)/shard_map/advect/pallas_call | solution.py:103
  91.5 2.4 %collective-permute-start.15 = (f32[8,2,512]{2,1,0:T(2,128)S(1)}, f32[8,2,512]{2,1,0:T(2,128)S(1)}, u32[]{:S(2)}, u32[]{:S(2)}) collective-permute-start(f32[8,2,512]{2,1,0:T(2,128)S(1)} %get-tuple-element.8), channel_id=1, source_target_pairs={{0,1},{1,2},{2,3},{3,0},{4,5},{5,6},{6,7},{7,4},{8,9},{9,10},{10,1... | collective-permute-start | bytes 98312 | tf_op jit(solution)/shard_map/ppermute | solution.py:123
  93.9 1.9 %collective-permute-done.14 = f32[8,2,512]{2,1,0:T(2,128)S(1)} collective-permute-done((f32[8,2,512]{2,1,0:T(2,128)S(1)}, f32[8,2,512]{2,1,0:T(2,128)S(1)}, u32[]{:S(2)}, u32[]{:S(2)}) %collective-permute-start.14) | collective-permute-done | bytes 32800 | tf_op jit(solution)/shard_map/ppermute | solution.py:123
  95.9 3.6 %collective-permute-start.17 = (f32[8,8,512]{2,1,0:T(8,128)S(1)}, f32[8,8,512]{2,1,0:T(8,128)S(1)}, u32[]{:S(2)}, u32[]{:S(2)}) collective-permute-start(f32[8,8,512]{2,1,0:T(8,128)S(1)} %pad_maximum_fusion.2.refs_7_), channel_id=1, source_target_pairs={{0,252},{4,0},{8,4},{12,8},{16,12},{20,16},{24,20},{28,24},{32,28}... | collective-permute-start | bytes 393224 | tf_op jit(solution)/shard_map/ppermute | solution.py:123
  100.9 13.2 %collective-permute-done.17.refs_8_ = f32[8,8,512]{2,1,0:T(8,128)S(1)} collective-permute-done((f32[8,8,512]{2,1,0:T(8,128)S(1)}, f32[8,8,512]{2,1,0:T(8,128)S(1)}, u32[]{:S(2)}, u32[]{:S(2)}) %collective-permute-start.17) | collective-permute-done | bytes 131104 | tf_op jit(solution)/shard_map/ppermute | solution.py:123
  114.1 5.3 %collective-permute-done.16.refs_6_ = f32[8,8,512]{2,1,0:T(8,128)S(1)} collective-permute-done((f32[8,8,512]{2,1,0:T(8,128)S(1)}, f32[8,8,512]{2,1,0:T(8,128)S(1)}, u32[]{:S(2)}, u32[]{:S(2)}) %collective-permute-start.16) | collective-permute-done | bytes 131104 | tf_op jit(solution)/shard_map/ppermute | solution.py:123
  120.7 8.7 %advect.6.refs_4_ = f32[8,128,512]{2,1,0:T(8,128)} custom-call(s32[32]{0:T(128)} %reshape_squeeze.26.refs_0_, s32[32]{0:T(128)} %reshape_squeeze.27.refs_1_, f32[192]{0:T(256)} %reshape.3.refs_2_, f32[8,128,512]{2,1,0:T(8,128)} %collective-permute-done.12.refs_3_, f32[8,128,512]{2,1,0:T(8,128)} %advect.5.refs_4_, f32[8,128,512]{2,1,0:T(8,128)} %copy-done.3, ...), custom_call_target="tpu_custom_call" | custom-call | tf_op jit(solution)/shard_map/advect/pallas_call | solution.py:103
  131.9 2.4 %collective-permute-start.21 = (f32[8,2,512]{2,1,0:T(2,128)S(1)}, f32[8,2,512]{2,1,0:T(2,128)S(1)}, u32[]{:S(2)}, u32[]{:S(2)}) collective-permute-start(f32[8,2,512]{2,1,0:T(2,128)S(1)} %get-tuple-element.6), channel_id=1, source_target_pairs={{0,1},{1,2},{2,3},{3,0},{4,5},{5,6},{6,7},{7,4},{8,9},{9,10},{10,1... | collective-permute-start | bytes 98312 | tf_op jit(solution)/shard_map/ppermute | solution.py:123
  134.3 1.9 %collective-permute-done.20 = f32[8,2,512]{2,1,0:T(2,128)S(1)} collective-permute-done((f32[8,2,512]{2,1,0:T(2,128)S(1)}, f32[8,2,512]{2,1,0:T(2,128)S(1)}, u32[]{:S(2)}, u32[]{:S(2)}) %collective-permute-start.20) | collective-permute-done | bytes 32800 | tf_op jit(solution)/shard_map/ppermute | solution.py:123
  136.3 3.6 %collective-permute-start.23 = (f32[8,8,512]{2,1,0:T(8,128)S(1)}, f32[8,8,512]{2,1,0:T(8,128)S(1)}, u32[]{:S(2)}, u32[]{:S(2)}) collective-permute-start(f32[8,8,512]{2,1,0:T(8,128)S(1)} %pad_maximum_fusion.3.refs_7_), channel_id=1, source_target_pairs={{0,252},{4,0},{8,4},{12,8},{16,12},{20,16},{24,20},{28,24},{32,28}... | collective-permute-start | bytes 393224 | tf_op jit(solution)/shard_map/ppermute | solution.py:123
  141.3 13.4 %collective-permute-done.23.refs_8_ = f32[8,8,512]{2,1,0:T(8,128)S(1)} collective-permute-done((f32[8,8,512]{2,1,0:T(8,128)S(1)}, f32[8,8,512]{2,1,0:T(8,128)S(1)}, u32[]{:S(2)}, u32[]{:S(2)}) %collective-permute-start.23) | collective-permute-done | bytes 131104 | tf_op jit(solution)/shard_map/ppermute | solution.py:123
  154.7 5.3 %collective-permute-done.22.refs_6_ = f32[8,8,512]{2,1,0:T(8,128)S(1)} collective-permute-done((f32[8,8,512]{2,1,0:T(8,128)S(1)}, f32[8,8,512]{2,1,0:T(8,128)S(1)}, u32[]{:S(2)}, u32[]{:S(2)}) %collective-permute-start.22) | collective-permute-done | bytes 131104 | tf_op jit(solution)/shard_map/ppermute | solution.py:123
  161.4 8.6 %advect.7 = f32[8,128,512]{2,1,0:T(8,128)} custom-call(s32[32]{0:T(128)} %reshape_squeeze.24.refs_0_, s32[32]{0:T(128)} %reshape_squeeze.25.refs_1_, f32[192]{0:T(256)} %reshape.3.refs_2_, f32[8,128,512]{2,1,0:T(8,128)} %collective-permute-done.18.refs_3_, f32[8,128,512]{2,1,0:T(8,128)} %advect.6.refs_4_, f32[8,128,512]{2,1,0:T(8,128)} %copy-done.1, ...), custom_call_target="tpu_custom_call" | custom-call | tf_op jit(solution)/shard_map/advect/pallas_call | solution.py:103
  (92 shorter events, 24.1 us)
Async XLA Ops:
  0.0 38.1 %collective-permute-start.1 = (f32[8,128,512]{2,1,0:T(8,128)}, f32[8,128,512]{2,1,0:T(8,128)S(1)}, u32[]{:S(2)}, u32[]{:S(2)}) collective-permute-start(f32[8,128,512]{2,1,0:T(8,128)} %refs_4_.1), channel_id=1, source_target_pairs={{0,252},{4,0},{8,4},{12,8},{16,12},{20,16},{24,20},{28,24},{32,28}... | collective-permute-start | bytes 6291464 | tf_op jit(solution)/shard_map/ppermute | solution.py:123
  7.7 30.4 %collective-permute-start = (f32[8,128,512]{2,1,0:T(8,128)}, f32[8,128,512]{2,1,0:T(8,128)}, u32[]{:S(2)}, u32[]{:S(2)}) collective-permute-start(f32[8,128,512]{2,1,0:T(8,128)} %refs_4_.1), channel_id=1, source_target_pairs={{0,4},{4,8},{8,12},{12,16},{16,20},{20,24},{24,28},{28,32},{32,36}... | collective-permute-start | bytes 6291464 | tf_op jit(solution)/shard_map/ppermute | solution.py:123
  8.8 6.5 %collective-permute-start.2 = (f32[8,2,512]{2,1,0:T(2,128)S(1)}, f32[8,2,512]{2,1,0:T(2,128)S(1)}, u32[]{:S(2)}, u32[]{:S(2)}) collective-permute-start(f32[8,2,512]{2,1,0:T(2,128)S(1)} %get-tuple-element.11), channel_id=1, source_target_pairs={{0,3},{1,0},{2,1},{3,2},{4,7},{5,4},{6,5},{7,6},{8,11},{9,8},{10,9... | collective-permute-start | bytes 98312 | tf_op jit(solution)/shard_map/ppermute | solution.py:123
  9.7 5.6 %collective-permute-start.3 = (f32[8,2,512]{2,1,0:T(2,128)S(1)}, f32[8,2,512]{2,1,0:T(2,128)S(1)}, u32[]{:S(2)}, u32[]{:S(2)}) collective-permute-start(f32[8,2,512]{2,1,0:T(2,128)S(1)} %get-tuple-element.12), channel_id=1, source_target_pairs={{0,1},{1,2},{2,3},{3,0},{4,5},{5,6},{6,7},{7,4},{8,9},{9,10},{10,1... | collective-permute-start | bytes 98312 | tf_op jit(solution)/shard_map/ppermute | solution.py:123
  15.3 17.6 %collective-permute-start.5 = (f32[8,8,512]{2,1,0:T(8,128)S(1)}, f32[8,8,512]{2,1,0:T(8,128)S(1)}, u32[]{:S(2)}, u32[]{:S(2)}) collective-permute-start(f32[8,8,512]{2,1,0:T(8,128)S(1)} %pad_maximum_fusion.refs_7_), channel_id=1, source_target_pairs={{0,252},{4,0},{8,4},{12,8},{16,12},{20,16},{24,20},{28,24},{32,28}... | collective-permute-start | bytes 393224 | tf_op jit(solution)/shard_map/ppermute | solution.py:123
  19.9 18.2 %collective-permute-start.4 = (f32[8,8,512]{2,1,0:T(8,128)S(1)}, f32[8,8,512]{2,1,0:T(8,128)S(1)}, u32[]{:S(2)}, u32[]{:S(2)}) collective-permute-start(f32[8,8,512]{2,1,0:T(8,128)S(1)} %pad_maximum_fusion.refs_7_), channel_id=1, source_target_pairs={{0,4},{4,8},{8,12},{12,16},{16,20},{20,24},{24,28},{28,32},{32,36}... | collective-permute-start | bytes 393224 | tf_op jit(solution)/shard_map/ppermute | solution.py:123
  48.2 30.6 %collective-permute-start.7 = (f32[8,128,512]{2,1,0:T(8,128)}, f32[8,128,512]{2,1,0:T(8,128)S(1)}, u32[]{:S(2)}, u32[]{:S(2)}) collective-permute-start(f32[8,128,512]{2,1,0:T(8,128)} %advect.4.refs_4_), channel_id=1, source_target_pairs={{0,252},{4,0},{8,4},{12,8},{16,12},{20,16},{24,20},{28,24},{32,28}... | collective-permute-start | bytes 6291464 | tf_op jit(solution)/shard_map/ppermute | solution.py:123
  48.3 30.5 %collective-permute-start.6 = (f32[8,128,512]{2,1,0:T(8,128)}, f32[8,128,512]{2,1,0:T(8,128)}, u32[]{:S(2)}, u32[]{:S(2)}) collective-permute-start(f32[8,128,512]{2,1,0:T(8,128)} %advect.4.refs_4_), channel_id=1, source_target_pairs={{0,4},{4,8},{8,12},{12,16},{16,20},{20,24},{24,28},{28,32},{32,36}... | collective-permute-start | bytes 6291464 | tf_op jit(solution)/shard_map/ppermute | solution.py:123
  49.8 5.2 %collective-permute-start.8 = (f32[8,2,512]{2,1,0:T(2,128)S(1)}, f32[8,2,512]{2,1,0:T(2,128)S(1)}, u32[]{:S(2)}, u32[]{:S(2)}) collective-permute-start(f32[8,2,512]{2,1,0:T(2,128)S(1)} %get-tuple-element.9), channel_id=1, source_target_pairs={{0,3},{1,0},{2,1},{3,2},{4,7},{5,4},{6,5},{7,6},{8,11},{9,8},{10,9... | collective-permute-start | bytes 98312 | tf_op jit(solution)/shard_map/ppermute | solution.py:123
  50.7 4.3 %collective-permute-start.9 = (f32[8,2,512]{2,1,0:T(2,128)S(1)}, f32[8,2,512]{2,1,0:T(2,128)S(1)}, u32[]{:S(2)}, u32[]{:S(2)}) collective-permute-start(f32[8,2,512]{2,1,0:T(2,128)S(1)} %get-tuple-element.10), channel_id=1, source_target_pairs={{0,1},{1,2},{2,3},{3,0},{4,5},{5,6},{6,7},{7,4},{8,9},{9,10},{10,1... | collective-permute-start | bytes 98312 | tf_op jit(solution)/shard_map/ppermute | solution.py:123
  55.1 18.4 %collective-permute-start.11 = (f32[8,8,512]{2,1,0:T(8,128)S(1)}, f32[8,8,512]{2,1,0:T(8,128)S(1)}, u32[]{:S(2)}, u32[]{:S(2)}) collective-permute-start(f32[8,8,512]{2,1,0:T(8,128)S(1)} %pad_maximum_fusion.1.refs_7_), channel_id=1, source_target_pairs={{0,252},{4,0},{8,4},{12,8},{16,12},{20,16},{24,20},{28,24},{32,28}... | collective-permute-start | bytes 393224 | tf_op jit(solution)/shard_map/ppermute | solution.py:123
  58.7 20.1 %collective-permute-start.10 = (f32[8,8,512]{2,1,0:T(8,128)S(1)}, f32[8,8,512]{2,1,0:T(8,128)S(1)}, u32[]{:S(2)}, u32[]{:S(2)}) collective-permute-start(f32[8,8,512]{2,1,0:T(8,128)S(1)} %pad_maximum_fusion.1.refs_7_), channel_id=1, source_target_pairs={{0,4},{4,8},{8,12},{12,16},{16,20},{20,24},{24,28},{28,32},{32,36}... | collective-permute-start | bytes 393224 | tf_op jit(solution)/shard_map/ppermute | solution.py:123
  88.8 30.6 %collective-permute-start.13 = (f32[8,128,512]{2,1,0:T(8,128)}, f32[8,128,512]{2,1,0:T(8,128)S(1)}, u32[]{:S(2)}, u32[]{:S(2)}) collective-permute-start(f32[8,128,512]{2,1,0:T(8,128)} %advect.5.refs_4_), channel_id=1, source_target_pairs={{0,252},{4,0},{8,4},{12,8},{16,12},{20,16},{24,20},{28,24},{32,28}... | collective-permute-start | bytes 6291464 | tf_op jit(solution)/shard_map/ppermute | solution.py:123
  88.9 30.5 %collective-permute-start.12 = (f32[8,128,512]{2,1,0:T(8,128)}, f32[8,128,512]{2,1,0:T(8,128)}, u32[]{:S(2)}, u32[]{:S(2)}) collective-permute-start(f32[8,128,512]{2,1,0:T(8,128)} %advect.5.refs_4_), channel_id=1, source_target_pairs={{0,4},{4,8},{8,12},{12,16},{16,20},{20,24},{24,28},{28,32},{32,36}... | collective-permute-start | bytes 6291464 | tf_op jit(solution)/shard_map/ppermute | solution.py:123
  90.4 5.4 %collective-permute-start.14 = (f32[8,2,512]{2,1,0:T(2,128)S(1)}, f32[8,2,512]{2,1,0:T(2,128)S(1)}, u32[]{:S(2)}, u32[]{:S(2)}) collective-permute-start(f32[8,2,512]{2,1,0:T(2,128)S(1)} %get-tuple-element.7), channel_id=1, source_target_pairs={{0,3},{1,0},{2,1},{3,2},{4,7},{5,4},{6,5},{7,6},{8,11},{9,8},{10,9... | collective-permute-start | bytes 98312 | tf_op jit(solution)/shard_map/ppermute | solution.py:123
  91.5 4.3 %collective-permute-start.15 = (f32[8,2,512]{2,1,0:T(2,128)S(1)}, f32[8,2,512]{2,1,0:T(2,128)S(1)}, u32[]{:S(2)}, u32[]{:S(2)}) collective-permute-start(f32[8,2,512]{2,1,0:T(2,128)S(1)} %get-tuple-element.8), channel_id=1, source_target_pairs={{0,1},{1,2},{2,3},{3,0},{4,5},{5,6},{6,7},{7,4},{8,9},{9,10},{10,1... | collective-permute-start | bytes 98312 | tf_op jit(solution)/shard_map/ppermute | solution.py:123
  95.9 18.2 %collective-permute-start.17 = (f32[8,8,512]{2,1,0:T(8,128)S(1)}, f32[8,8,512]{2,1,0:T(8,128)S(1)}, u32[]{:S(2)}, u32[]{:S(2)}) collective-permute-start(f32[8,8,512]{2,1,0:T(8,128)S(1)} %pad_maximum_fusion.2.refs_7_), channel_id=1, source_target_pairs={{0,252},{4,0},{8,4},{12,8},{16,12},{20,16},{24,20},{28,24},{32,28}... | collective-permute-start | bytes 393224 | tf_op jit(solution)/shard_map/ppermute | solution.py:123
  99.4 19.9 %collective-permute-start.16 = (f32[8,8,512]{2,1,0:T(8,128)S(1)}, f32[8,8,512]{2,1,0:T(8,128)S(1)}, u32[]{:S(2)}, u32[]{:S(2)}) collective-permute-start(f32[8,8,512]{2,1,0:T(8,128)S(1)} %pad_maximum_fusion.2.refs_7_), channel_id=1, source_target_pairs={{0,4},{4,8},{8,12},{12,16},{16,20},{20,24},{24,28},{28,32},{32,36}... | collective-permute-start | bytes 393224 | tf_op jit(solution)/shard_map/ppermute | solution.py:123
  129.4 30.6 %collective-permute-start.19 = (f32[8,128,512]{2,1,0:T(8,128)}, f32[8,128,512]{2,1,0:T(8,128)S(1)}, u32[]{:S(2)}, u32[]{:S(2)}) collective-permute-start(f32[8,128,512]{2,1,0:T(8,128)} %advect.6.refs_4_), channel_id=1, source_target_pairs={{0,252},{4,0},{8,4},{12,8},{16,12},{20,16},{24,20},{28,24},{32,28}... | collective-permute-start | bytes 6291464 | tf_op jit(solution)/shard_map/ppermute | solution.py:123
  129.5 30.5 %collective-permute-start.18 = (f32[8,128,512]{2,1,0:T(8,128)}, f32[8,128,512]{2,1,0:T(8,128)}, u32[]{:S(2)}, u32[]{:S(2)}) collective-permute-start(f32[8,128,512]{2,1,0:T(8,128)} %advect.6.refs_4_), channel_id=1, source_target_pairs={{0,4},{4,8},{8,12},{12,16},{16,20},{20,24},{24,28},{28,32},{32,36}... | collective-permute-start | bytes 6291464 | tf_op jit(solution)/shard_map/ppermute | solution.py:123
  131.0 5.2 %collective-permute-start.20 = (f32[8,2,512]{2,1,0:T(2,128)S(1)}, f32[8,2,512]{2,1,0:T(2,128)S(1)}, u32[]{:S(2)}, u32[]{:S(2)}) collective-permute-start(f32[8,2,512]{2,1,0:T(2,128)S(1)} %get-tuple-element.5), channel_id=1, source_target_pairs={{0,3},{1,0},{2,1},{3,2},{4,7},{5,4},{6,5},{7,6},{8,11},{9,8},{10,9... | collective-permute-start | bytes 98312 | tf_op jit(solution)/shard_map/ppermute | solution.py:123
  131.9 4.3 %collective-permute-start.21 = (f32[8,2,512]{2,1,0:T(2,128)S(1)}, f32[8,2,512]{2,1,0:T(2,128)S(1)}, u32[]{:S(2)}, u32[]{:S(2)}) collective-permute-start(f32[8,2,512]{2,1,0:T(2,128)S(1)} %get-tuple-element.6), channel_id=1, source_target_pairs={{0,1},{1,2},{2,3},{3,0},{4,5},{5,6},{6,7},{7,4},{8,9},{9,10},{10,1... | collective-permute-start | bytes 98312 | tf_op jit(solution)/shard_map/ppermute | solution.py:123
  136.3 18.4 %collective-permute-start.23 = (f32[8,8,512]{2,1,0:T(8,128)S(1)}, f32[8,8,512]{2,1,0:T(8,128)S(1)}, u32[]{:S(2)}, u32[]{:S(2)}) collective-permute-start(f32[8,8,512]{2,1,0:T(8,128)S(1)} %pad_maximum_fusion.3.refs_7_), channel_id=1, source_target_pairs={{0,252},{4,0},{8,4},{12,8},{16,12},{20,16},{24,20},{28,24},{32,28}... | collective-permute-start | bytes 393224 | tf_op jit(solution)/shard_map/ppermute | solution.py:123
  139.9 20.1 %collective-permute-start.22 = (f32[8,8,512]{2,1,0:T(8,128)S(1)}, f32[8,8,512]{2,1,0:T(8,128)S(1)}, u32[]{:S(2)}, u32[]{:S(2)}) collective-permute-start(f32[8,8,512]{2,1,0:T(8,128)S(1)} %pad_maximum_fusion.3.refs_7_), channel_id=1, source_target_pairs={{0,4},{4,8},{8,12},{12,16},{16,20},{20,24},{24,28},{28,32},{32,36}... | collective-permute-start | bytes 393224 | tf_op jit(solution)/shard_map/ppermute | solution.py:123
  (16 other events, 123.1 us)

commit v2 on v0

v2 whole, which is shorter than its diff:
```python
import jax
import jax.numpy as jnp
from jax import lax
from jax.experimental import pallas as pl
from jax.experimental.pallas import tpu as pltpu
from jax.sharding import PartitionSpec as P


REACH = 8
LANES = 128
TILE = 8
MARGIN = 8


def cubic_weights(shares):
    return (
        -shares * (shares - 1.0) * (shares - 2.0) / 6.0,
        (shares + 1.0) * (shares - 1.0) * (shares - 2.0) / 2.0,
        -(shares + 1.0) * shares * (shares - 2.0) / 2.0,
        (shares + 1.0) * shares * (shares - 1.0) / 6.0,
    )


def weight_table(fractions):
    parts = [jnp.stack(cubic_weights(1.0 - fractions[:, axis]), axis=1) for axis in range(3)]
    return jnp.concatenate(parts, axis=1).reshape(-1)


def sweep(step, pieces, moves, tiles, targets, tags, table, ends=(), finish=None):
    planes, _, width = pieces[0][1].shape
    blocks = width // LANES
    inputs = [part for piece in pieces for part in piece]
    if finish:
        whole, first, middle = finish
        inputs.append(middle)
        after = first + middle.shape[1]

    def body(tag_ref, tab_ref, *refs):
        sources = refs[: len(inputs)]
        outputs = refs[len(inputs) : len(inputs) + 1 + len(ends)]
        win, line, *more = refs[len(inputs) + 1 + len(ends) :]
        out_ref = outputs[0]
        if finish:
            out_ref, sems = more
            last = pltpu.make_async_copy(sources[-1], outputs[0].at[:, pl.ds(first, after - first), :], sems.at[0])
            last.start()

        def drains(k):
            return [
                pltpu.make_async_copy(
                    out_ref.at[k, pl.ds(row, height), :], outputs[0].at[k, pl.ds(row, height), :], sems.at[1 + 2 * k + i]
                )
                for i, (row, height) in enumerate([(0, first), (after, whole - after)])
            ]

        def fill(p, carry):
            for piece, row, at, height in moves:
                for part in range(3):
                    win[part * planes + p, pl.ds(at, height), :] = sources[3 * piece + part][p, pl.ds(row, height), :]
            return carry

        lax.fori_loop(0, planes, fill, 0)
        lane = lax.broadcasted_iota(jnp.int32, (TILE, LANES), 1)
        from_right = lane < LANES // 2
        last_two = lane >= LANES - 2
        last_one = lane >= LANES - 1
        first_one = lane == 0

        def plane(k, carry):
            for b in range(blocks):
                here = pl.ds(b * LANES, LANES)
                left = pl.ds(((b - 1) % blocks) * LANES, LANES)
                right = pl.ds(((b + 1) % blocks) * LANES, LANES)
                tag = (step * planes + k) * blocks + b
                base = k - tag_ref[0, tag] + (REACH - 2)
                entry = tag_ref[1, tag] * 12
                cz = [tab_ref[entry + n] for n in range(4)]
                cx = [tab_ref[entry + 4 + n] for n in range(4)]
                cy = [tab_ref[entry + 8 + n] for n in range(4)]
                for t in range(tiles):
                    rows = pl.ds(t * TILE, TILE)
                    mid = None
                    edge = None
                    for n in range(4):
                        m = cz[n] * win[base + n, rows, here]
                        e = cz[n] * jnp.where(from_right, win[base + n, rows, right], win[base + n, rows, left])
                        mid = m if mid is None else mid + m
                        edge = e if edge is None else edge + e
                    y = cy[2] * mid
                    y = y + cy[0] * pltpu.roll(jnp.where(last_two, edge, mid), 2, 1)
                    y = y + cy[1] * pltpu.roll(jnp.where(last_one, edge, mid), 1, 1)
                    y = y + cy[3] * pltpu.roll(jnp.where(first_one, edge, mid), LANES - 1, 1)
                    line[b, rows, :] = y
                for t, row in targets:
                    acc = cx[0] * line[b, pl.ds(t * TILE - 2, TILE), :]
                    for n in range(1, 4):
                        acc = acc + cx[n] * line[b, pl.ds(t * TILE - 2 + n, TILE), :]
                    out_ref[k, pl.ds(row, TILE), here] = acc
                    for end, end_ref in zip(ends, outputs[1:]):
                        if t == end:
                            end_ref[k, :, here] = acc
            if finish:
                for copy in drains(k):
                    copy.start()
            return carry

        lax.fori_loop(0, planes, plane, 0)
        if finish:
            last.wait()
            for k in range(planes):
                for copy in drains(k):
                    copy.wait()

    inside = pl.BlockSpec(memory_space=pltpu.VMEM)
    scalars = pl.BlockSpec(memory_space=pltpu.SMEM)
    scratch = [
        pltpu.VMEM((3 * planes, tiles * TILE, width), jnp.float32),
        pltpu.VMEM((blocks, tiles * TILE, LANES), jnp.float32),
    ]
    if finish:
        out_shape = jax.ShapeDtypeStruct((planes, whole, width), jnp.float32)
        out_specs = pl.BlockSpec(memory_space=pl.ANY)
        scratch += [
            pltpu.VMEM((planes, whole, width), jnp.float32),
            pltpu.SemaphoreType.DMA((1 + 2 * planes,)),
        ]
    else:
        height = max(row for _, row in targets) + TILE
        out_shape = [jax.ShapeDtypeStruct((planes, height, width), jnp.float32)]
        out_shape += [jax.ShapeDtypeStruct((planes, TILE, width), jnp.float32)] * len(ends)
        out_specs = [inside] * len(out_shape)
    return pl.pallas_call(
        body,
        out_shape=out_shape,
        in_specs=[scalars] * 2 + [inside] * len(inputs),
        out_specs=out_specs,
        scratch_shapes=scratch,
        compiler_params=pltpu.CompilerParams(vmem_limit_bytes=14 << 20),
        name="sweep",
    )(tags, table, *inputs)


def shifted(x, axis, by):
    devices = lax.axis_size(axis)
    return lax.ppermute(x, axis, [(i, (i + by) % devices) for i in range(devices)])


def stacked(x):
    up = shifted(x, "gz", 1)
    down = shifted(x, "gz", -1)
    return up, x, down


def rim_of(first, last):
    above = shifted(last, "xy", 1)
    below = shifted(first, "xy", -1)
    row = lax.broadcasted_iota(jnp.int32, above.shape, 1)
    return jnp.where(row < TILE // 2, below, above)


def advance(image, offsets, frac_index, fractions):
    rows = image.shape[1]
    steps = offsets.shape[0]
    table = weight_table(fractions)
    tags = jnp.stack([offsets.reshape(-1), frac_index.reshape(-1)])
    margin = MARGIN
    centre = image[:, margin : rows - margin]
    first, last = image[:, :TILE], image[:, rows - TILE :]
    outer = None
    for step in range(steps):
        rim = rim_of(first, last)
        if outer is None:
            outer = jnp.concatenate([image[:, rows - margin :], rim, image[:, :margin]], axis=1)
        else:
            outer = lax.dynamic_update_slice(outer, rim, (0, margin, 0))
        inner = stacked(centre)
        outside = stacked(outer)
        tall = rows - 2 * margin
        many = margin // TILE
        margin += TILE
        (centre,) = sweep(
            step, [inner], [(0, 0, 0, tall)], tall // TILE,
            [(t, (t - 1) * TILE) for t in range(1, tall // TILE - 1)], tags, table,
        )
        moves = [(0, tall - 16, 0, 16), (1, 0, 16, 2 * margin - TILE), (0, 0, 8 + 2 * margin, 16)]
        upper, lower = range(1, many + 2), range(many + 3, 2 * many + 4)
        if step < steps - 1:
            outer, last, first = sweep(
                step, [inner, outside], moves, 2 * many + 5,
                [(t, (t - 1) * TILE) for t in (*upper, *lower)], tags, table,
                ends=(many + 1, many + 3),
            )
        else:
            targets = [(t, rows - margin + (t - 1) * TILE) for t in upper]
            targets += [(t, (t - many - 3) * TILE) for t in lower]
            image = sweep(
                step, [inner, outside], moves, 2 * many + 5, targets, tags, table,
                finish=(rows, margin, centre),
            )
    return image


def solution(mesh):
    in_specs = (P("gz", "xy", None), P(None, "gz", "xy", None), P(None, "gz", "xy", None), P())
    out_specs = P("gz", "xy", None)
    return jax.shard_map(advance, mesh=mesh, in_specs=in_specs, out_specs=out_specs, check_vma=False)
```

time: 244 us -> 167 us (0.68)
  the two profiles are of different devices: /device:TPU:123 before, /device:TPU:2 now
where the time goes in v2:
time: 167 us
  waiting for transfers between devices  100 us (60%)
  starting transfers between devices  33.9 us (20%)
  Pallas kernels  28.1 us (17%)
  local copies, waits for them, and re-layouts  3.39 us (2%)
    ppermute x24, waiting for transfers between devices, shifted(): lax.ppermute(x, axis, [(i, (i + by) % devices) for i in range(devices)])  100 us
    ppermute x24, starting transfers between devices, shifted(): lax.ppermute(x, axis, [(i, (i + by) % devices) for i in range(devices)])  33.9 us
    pallas_call x8, Pallas kernels, sweep(): pl.pallas_call(body, out_shape=out_shape, in_specs=[scalars] * 2 + [insid...  28.1 us
  transfers between devices with their start and end apart: 24, of which 15 were waited for; matrix products, arithmetic and copies ran while one was open for 1% of the time, Pallas kernels for 12%

profile of v2, /device:TPU:2, one launch (start us, length us, event | category | flops | bytes accessed | tf_op | source)
XLA Modules:
  0.0 166.6 jit_solution(5050449779862055754)
XLA Ops:
  1.8 7.8 %collective-permute-start.1 = (f32[8,112,512]{2,1,0:T(8,128)S(1)}, f32[8,112,512]{2,1,0:T(8,128)}, u32[]{:S(2)}, u32[]{:S(2)}) collective-permute-start(f32[8,112,512]{2,1,0:T(8,128)S(1)} %slice.23.refs_1_), channel_id=1, source_target_pairs={{0,252},{4,0},{8,4},{12,8},{16,12},{20,16},{24,20},{28,24},{32,28}... | collective-permute-start | bytes 5505032 | tf_op jit(solution)/shard_map/ppermute | solution.py:145
  13.4 16.9 %collective-permute-done.1.refs_2_ = f32[8,112,512]{2,1,0:T(8,128)} collective-permute-done((f32[8,112,512]{2,1,0:T(8,128)S(1)}, f32[8,112,512]{2,1,0:T(8,128)}, u32[]{:S(2)}, u32[]{:S(2)}) %collective-permute-start.1) | collective-permute-done | bytes 1835040 | tf_op jit(solution)/shard_map/ppermute | solution.py:145
  30.4 5.3 %collective-permute-done.refs_0_ = f32[8,112,512]{2,1,0:T(8,128)} collective-permute-done((f32[8,112,512]{2,1,0:T(8,128)S(1)}, f32[8,112,512]{2,1,0:T(8,128)}, u32[]{:S(2)}, u32[]{:S(2)}) %collective-permute-start) | collective-permute-done | bytes 1835040 | tf_op jit(solution)/shard_map/ppermute | solution.py:145
  35.7 5.3 %sweep.8.refs_1_ = f32[8,96,512]{2,1,0:T(8,128)S(1)} custom-call(s32[2,128]{1,0:T(2,128)S(1)} %pad_add_fusion.tag_ref, f32[192]{0:T(256)S(1)} %reshape.3.tab_ref, f32[8,112,512]{2,1,0:T(8,128)} %collective-permute-done.refs_0_, f32[8,112,512]{2,1,0:T(8,128)S(1)} %slice.23.refs_1_, f32[8,112,512]{2,1,0:T(8,128)} %collective-permute-done.1.refs_2_), custom_call_target="tpu_custom_call" | custom-call | tf_op jit(solution)/shard_map/sweep/pallas_call | solution.py:132
  41.7 4.7 %collective-permute-start.11 = (f32[8,24,512]{2,1,0:T(8,128)S(1)}, f32[8,24,512]{2,1,0:T(8,128)S(1)}, u32[]{:S(2)}, u32[]{:S(2)}) collective-permute-start(f32[8,24,512]{2,1,0:T(8,128)S(1)} %pad_maximum_fusion.refs_4_), channel_id=1, source_target_pairs={{0,252},{4,0},{8,4},{12,8},{16,12},{20,16},{24,20},{28,24},{32,28}... | collective-permute-start | bytes 1179656 | tf_op jit(solution)/shard_map/ppermute | solution.py:145
  46.4 16.8 %collective-permute-done.11.refs_5_ = f32[8,24,512]{2,1,0:T(8,128)S(1)} collective-permute-done((f32[8,24,512]{2,1,0:T(8,128)S(1)}, f32[8,24,512]{2,1,0:T(8,128)S(1)}, u32[]{:S(2)}, u32[]{:S(2)}) %collective-permute-start.11) | collective-permute-done | bytes 393248 | tf_op jit(solution)/shard_map/ppermute | solution.py:145
  63.2 5.3 %collective-permute-done.10.refs_3_ = f32[8,24,512]{2,1,0:T(8,128)S(1)} collective-permute-done((f32[8,24,512]{2,1,0:T(8,128)S(1)}, f32[8,24,512]{2,1,0:T(8,128)S(1)}, u32[]{:S(2)}, u32[]{:S(2)}) %collective-permute-start.10) | collective-permute-done | bytes 393248 | tf_op jit(solution)/shard_map/ppermute | solution.py:145
  68.5 3.9 %sweep.11 = (f32[8,40,512]{2,1,0:T(8,128)S(1)}, f32[8,8,512]{2,1,0:T(8,128)S(1)}, f32[8,8,512]{2,1,0:T(8,128)S(1)}) custom-call(s32[2,128]{1,0:T(2,128)S(1)} %pad_add_fusion.tag_ref, f32[192]{0:T(256)S(1)} %reshape.3.tab_ref, f32[8,112,512]{2,1,0:T(8,128)} %collective-permute-done.refs_0_, f32[8,112,512]{2,1,0:T(8,128)S(1)} %slice.23.refs_1_, ...), custom_call_target="tpu_custom_call" | custom-call | tf_op jit(solution)/shard_map/sweep/pallas_call | solution.py:132
  74.5 2.9 %collective-permute-done.12 = f32[8,8,512]{2,1,0:T(8,128)S(1)} collective-permute-done((f32[8,8,512]{2,1,0:T(8,128)S(1)}, f32[8,8,512]{2,1,0:T(8,128)S(1)}, u32[]{:S(2)}, u32[]{:S(2)}) %collective-permute-start.12) | collective-permute-done | bytes 131104 | tf_op jit(solution)/shard_map/ppermute | solution.py:145
  79.4 3.3 %sweep.9.refs_1_ = f32[8,80,512]{2,1,0:T(8,128)S(1)} custom-call(s32[2,128]{1,0:T(2,128)S(1)} %pad_add_fusion.tag_ref, f32[192]{0:T(256)S(1)} %reshape.3.tab_ref, f32[8,96,512]{2,1,0:T(8,128)S(1)} %collective-permute-done.2.refs_0_, f32[8,96,512]{2,1,0:T(8,128)S(1)} %sweep.8.refs_1_, f32[8,96,512]{2,1,0:T(8,128)S(1)} %collective-permute-done.3.refs_2_), custom_call_target="tpu_custom_call" | custom-call | tf_op jit(solution)/shard_map/sweep/pallas_call | solution.py:132
  82.7 4.7 %collective-permute-start.5 = (f32[8,80,512]{2,1,0:T(8,128)S(1)}, f32[8,80,512]{2,1,0:T(8,128)S(1)}, u32[]{:S(2)}, u32[]{:S(2)}) collective-permute-start(f32[8,80,512]{2,1,0:T(8,128)S(1)} %sweep.9.refs_1_), channel_id=1, source_target_pairs={{0,252},{4,0},{8,4},{12,8},{16,12},{20,16},{24,20},{28,24},{32,28}... | collective-permute-start | bytes 3932168 | tf_op jit(solution)/shard_map/ppermute | solution.py:145
  87.5 4.8 %collective-permute-done.14.refs_3_ = f32[8,40,512]{2,1,0:T(8,128)S(1)} collective-permute-done((f32[8,40,512]{2,1,0:T(8,128)S(1)}, f32[8,40,512]{2,1,0:T(8,128)S(1)}, u32[]{:S(2)}, u32[]{:S(2)}) %collective-permute-start.14) | collective-permute-done | bytes 655392 | tf_op jit(solution)/shard_map/ppermute | solution.py:145
  92.3 2.7 %sweep.12 = (f32[8,56,512]{2,1,0:T(8,128)S(1)}, f32[8,8,512]{2,1,0:T(8,128)S(1)}, f32[8,8,512]{2,1,0:T(8,128)S(1)}) custom-call(s32[2,128]{1,0:T(2,128)S(1)} %pad_add_fusion.tag_ref, f32[192]{0:T(256)S(1)} %reshape.3.tab_ref, f32[8,96,512]{2,1,0:T(8,128)S(1)} %collective-permute-done.2.refs_0_, f32[8,96,512]{2,1,0:T(8,128)S(1)} %sweep.8.refs_1_, ...), custom_call_target="tpu_custom_call" | custom-call | tf_op jit(solution)/shard_map/sweep/pallas_call | solution.py:132
  95.0 3.3 %collective-permute-start.16 = (f32[8,8,512]{2,1,0:T(8,128)S(1)}, f32[8,8,512]{2,1,0:T(8,128)S(1)}, u32[]{:S(2)}, u32[]{:S(2)}) collective-permute-start(f32[8,8,512]{2,1,0:T(8,128)S(1)} %get-tuple-element.18), channel_id=1, source_target_pairs={{0,3},{1,0},{2,1},{3,2},{4,7},{5,4},{6,5},{7,6},{8,11},{9,8},{10,9... | collective-permute-start | bytes 393224 | tf_op jit(solution)/shard_map/ppermute | solution.py:145
  98.3 2.5 %collective-permute-done.16 = f32[8,8,512]{2,1,0:T(8,128)S(1)} collective-permute-done((f32[8,8,512]{2,1,0:T(8,128)S(1)}, f32[8,8,512]{2,1,0:T(8,128)S(1)}, u32[]{:S(2)}, u32[]{:S(2)}) %collective-permute-start.16) | collective-permute-done | bytes 131104 | tf_op jit(solution)/shard_map/ppermute | solution.py:145
  104.0 10.4 %collective-permute-done.19.refs_5_ = f32[8,56,512]{2,1,0:T(8,128)S(1)} collective-permute-done((f32[8,56,512]{2,1,0:T(8,128)S(1)}, f32[8,56,512]{2,1,0:T(8,128)S(1)}, u32[]{:S(2)}, u32[]{:S(2)}) %collective-permute-start.19) | collective-permute-done | bytes 917536 | tf_op jit(solution)/shard_map/ppermute | solution.py:145
  114.4 5.3 %collective-permute-done.18.refs_3_ = f32[8,56,512]{2,1,0:T(8,128)S(1)} collective-permute-done((f32[8,56,512]{2,1,0:T(8,128)S(1)}, f32[8,56,512]{2,1,0:T(8,128)S(1)}, u32[]{:S(2)}, u32[]{:S(2)}) %collective-permute-start.18) | collective-permute-done | bytes 917536 | tf_op jit(solution)/shard_map/ppermute | solution.py:145
  119.7 3.1 %sweep.13 = (f32[8,72,512]{2,1,0:T(8,128)S(1)}, f32[8,8,512]{2,1,0:T(8,128)S(1)}, f32[8,8,512]{2,1,0:T(8,128)S(1)}) custom-call(s32[2,128]{1,0:T(2,128)S(1)} %pad_add_fusion.tag_ref, f32[192]{0:T(256)S(1)} %reshape.3.tab_ref, f32[8,80,512]{2,1,0:T(8,128)S(1)} %collective-permute-done.4.refs_0_, f32[8,80,512]{2,1,0:T(8,128)S(1)} %sweep.9.refs_1_, ...), custom_call_target="tpu_custom_call" | custom-call | tf_op jit(solution)/shard_map/sweep/pallas_call | solution.py:132
  124.9 2.9 %collective-permute-done.20 = f32[8,8,512]{2,1,0:T(8,128)S(1)} collective-permute-done((f32[8,8,512]{2,1,0:T(8,128)S(1)}, f32[8,8,512]{2,1,0:T(8,128)S(1)}, u32[]{:S(2)}, u32[]{:S(2)}) %collective-permute-start.20) | collective-permute-done | bytes 131104 | tf_op jit(solution)/shard_map/ppermute | solution.py:145
  129.8 3.0 %sweep.10.refs_1_ = f32[8,64,512]{2,1,0:T(8,128)S(1)} custom-call(s32[2,128]{1,0:T(2,128)S(1)} %pad_add_fusion.tag_ref, f32[192]{0:T(256)S(1)} %reshape.3.tab_ref, f32[8,80,512]{2,1,0:T(8,128)S(1)} %collective-permute-done.4.refs_0_, f32[8,80,512]{2,1,0:T(8,128)S(1)} %sweep.9.refs_1_, f32[8,80,512]{2,1,0:T(8,128)S(1)} %collective-permute-done.5.refs_2_), custom_call_target="tpu_custom_call" | custom-call | tf_op jit(solution)/shard_map/sweep/pallas_call | solution.py:132
  132.8 4.7 %collective-permute-start.7 = (f32[8,64,512]{2,1,0:T(8,128)S(1)}, f32[8,64,512]{2,1,0:T(8,128)S(1)}, u32[]{:S(2)}, u32[]{:S(2)}) collective-permute-start(f32[8,64,512]{2,1,0:T(8,128)S(1)} %sweep.10.refs_1_), channel_id=1, source_target_pairs={{0,252},{4,0},{8,4},{12,8},{16,12},{20,16},{24,20},{28,24},{32,28}... | collective-permute-start | bytes 3145736 | tf_op jit(solution)/shard_map/ppermute | solution.py:145
  137.5 16.8 %collective-permute-done.7.refs_2_ = f32[8,64,512]{2,1,0:T(8,128)S(1)} collective-permute-done((f32[8,64,512]{2,1,0:T(8,128)S(1)}, f32[8,64,512]{2,1,0:T(8,128)S(1)}, u32[]{:S(2)}, u32[]{:S(2)}) %collective-permute-start.7) | collective-permute-done | bytes 1048608 | tf_op jit(solution)/shard_map/ppermute | solution.py:145
  154.3 5.3 %collective-permute-done.6.refs_0_ = f32[8,64,512]{2,1,0:T(8,128)S(1)} collective-permute-done((f32[8,64,512]{2,1,0:T(8,128)S(1)}, f32[8,64,512]{2,1,0:T(8,128)S(1)}, u32[]{:S(2)}, u32[]{:S(2)}) %collective-permute-start.6) | collective-permute-done | bytes 1048608 | tf_op jit(solution)/shard_map/ppermute | solution.py:145
  162.1 4.4 %sweep.15 = f32[8,128,512]{2,1,0:T(8,128)} custom-call(s32[2,128]{1,0:T(2,128)S(1)} %pad_add_fusion.tag_ref, f32[192]{0:T(256)S(1)} %reshape.3.tab_ref, f32[8,64,512]{2,1,0:T(8,128)S(1)} %collective-permute-done.6.refs_0_, f32[8,64,512]{2,1,0:T(8,128)S(1)} %sweep.10.refs_1_, f32[8,64,512]{2,1,0:T(8,128)S(1)} %collective-permute-done.7.refs_2_, ...), custom_call_target="tpu_custom_call" | custom-call | tf_op jit(solution)/shard_map/sweep/pallas_call | solution.py:132
  (55 shorter events, 19.9 us)
Async XLA Ops:
  1.8 28.6 %collective-permute-start.1 = (f32[8,112,512]{2,1,0:T(8,128)S(1)}, f32[8,112,512]{2,1,0:T(8,128)}, u32[]{:S(2)}, u32[]{:S(2)}) collective-permute-start(f32[8,112,512]{2,1,0:T(8,128)S(1)} %slice.23.refs_1_), channel_id=1, source_target_pairs={{0,252},{4,0},{8,4},{12,8},{16,12},{20,16},{24,20},{28,24},{32,28}... | collective-permute-start | bytes 5505032 | tf_op jit(solution)/shard_map/ppermute | solution.py:145
  9.6 26.1 %collective-permute-start = (f32[8,112,512]{2,1,0:T(8,128)S(1)}, f32[8,112,512]{2,1,0:T(8,128)}, u32[]{:S(2)}, u32[]{:S(2)}) collective-permute-start(f32[8,112,512]{2,1,0:T(8,128)S(1)} %slice.23.refs_1_), channel_id=1, source_target_pairs={{0,4},{4,8},{8,12},{12,16},{16,20},{20,24},{24,28},{28,32},{32,36}... | collective-permute-start | bytes 5505032 | tf_op jit(solution)/shard_map/ppermute | solution.py:145
  10.6 31.0 %collective-permute-start.9 = (f32[8,8,512]{2,1,0:T(8,128)S(1)}, f32[8,8,512]{2,1,0:T(8,128)S(1)}, u32[]{:S(2)}, u32[]{:S(2)}) collective-permute-start(f32[8,8,512]{2,1,0:T(8,128)S(1)} %get-tuple-element.23), channel_id=1, source_target_pairs={{0,1},{1,2},{2,3},{3,0},{4,5},{5,6},{6,7},{7,4},{8,9},{9,10},{10,1... | collective-permute-start | bytes 393224 | tf_op jit(solution)/shard_map/ppermute | solution.py:145
  12.2 29.4 %collective-permute-start.8 = (f32[8,8,512]{2,1,0:T(8,128)S(1)}, f32[8,8,512]{2,1,0:T(8,128)S(1)}, u32[]{:S(2)}, u32[]{:S(2)}) collective-permute-start(f32[8,8,512]{2,1,0:T(8,128)S(1)} %get-tuple-element.24), channel_id=1, source_target_pairs={{0,3},{1,0},{2,1},{3,2},{4,7},{5,4},{6,5},{7,6},{8,11},{9,8},{10,9... | collective-permute-start | bytes 393224 | tf_op jit(solution)/shard_map/ppermute | solution.py:145
  41.0 38.4 %collective-permute-start.3 = (f32[8,96,512]{2,1,0:T(8,128)S(1)}, f32[8,96,512]{2,1,0:T(8,128)S(1)}, u32[]{:S(2)}, u32[]{:S(2)}) collective-permute-start(f32[8,96,512]{2,1,0:T(8,128)S(1)} %sweep.8.refs_1_), channel_id=1, source_target_pairs={{0,252},{4,0},{8,4},{12,8},{16,12},{20,16},{24,20},{28,24},{32,28}... | collective-permute-start | bytes 4718600 | tf_op jit(solution)/shard_map/ppermute | solution.py:145
  41.1 38.3 %collective-permute-start.2 = (f32[8,96,512]{2,1,0:T(8,128)S(1)}, f32[8,96,512]{2,1,0:T(8,128)S(1)}, u32[]{:S(2)}, u32[]{:S(2)}) collective-permute-start(f32[8,96,512]{2,1,0:T(8,128)S(1)} %sweep.8.refs_1_), channel_id=1, source_target_pairs={{0,4},{4,8},{8,12},{12,16},{16,20},{20,24},{24,28},{28,32},{32,36}... | collective-permute-start | bytes 4718600 | tf_op jit(solution)/shard_map/ppermute | solution.py:145
  41.7 21.5 %collective-permute-start.11 = (f32[8,24,512]{2,1,0:T(8,128)S(1)}, f32[8,24,512]{2,1,0:T(8,128)S(1)}, u32[]{:S(2)}, u32[]{:S(2)}) collective-permute-start(f32[8,24,512]{2,1,0:T(8,128)S(1)} %pad_maximum_fusion.refs_4_), channel_id=1, source_target_pairs={{0,252},{4,0},{8,4},{12,8},{16,12},{20,16},{24,20},{28,24},{32,28}... | collective-permute-start | bytes 1179656 | tf_op jit(solution)/shard_map/ppermute | solution.py:145
  46.4 22.1 %collective-permute-start.10 = (f32[8,24,512]{2,1,0:T(8,128)S(1)}, f32[8,24,512]{2,1,0:T(8,128)S(1)}, u32[]{:S(2)}, u32[]{:S(2)}) collective-permute-start(f32[8,24,512]{2,1,0:T(8,128)S(1)} %pad_maximum_fusion.refs_4_), channel_id=1, source_target_pairs={{0,4},{4,8},{8,12},{12,16},{16,20},{20,24},{24,28},{28,32},{32,36}... | collective-permute-start | bytes 1179656 | tf_op jit(solution)/shard_map/ppermute | solution.py:145
  72.4 5.0 %collective-permute-start.12 = (f32[8,8,512]{2,1,0:T(8,128)S(1)}, f32[8,8,512]{2,1,0:T(8,128)S(1)}, u32[]{:S(2)}, u32[]{:S(2)}) collective-permute-start(f32[8,8,512]{2,1,0:T(8,128)S(1)} %get-tuple-element.15), channel_id=1, source_target_pairs={{0,3},{1,0},{2,1},{3,2},{4,7},{5,4},{6,5},{7,6},{8,11},{9,8},{10,9... | collective-permute-start | bytes 393224 | tf_op jit(solution)/shard_map/ppermute | solution.py:145
  73.0 5.7 %collective-permute-start.13 = (f32[8,8,512]{2,1,0:T(8,128)S(1)}, f32[8,8,512]{2,1,0:T(8,128)S(1)}, u32[]{:S(2)}, u32[]{:S(2)}) collective-permute-start(f32[8,8,512]{2,1,0:T(8,128)S(1)} %get-tuple-element.16), channel_id=1, source_target_pairs={{0,1},{1,2},{2,3},{3,0},{4,5},{5,6},{6,7},{7,4},{8,9},{9,10},{10,1... | collective-permute-start | bytes 393224 | tf_op jit(solution)/shard_map/ppermute | solution.py:145
  78.8 8.6 %collective-permute-start.15 = (f32[8,40,512]{2,1,0:T(8,128)S(1)}, f32[8,40,512]{2,1,0:T(8,128)S(1)}, u32[]{:S(2)}, u32[]{:S(2)}) collective-permute-start(f32[8,40,512]{2,1,0:T(8,128)S(1)} %select_dynamic-update-slice_fusion.2.refs_4_), channel_id=1, source_target_pairs={{0,252},{4,0},{8,4},{12,8},{16,12},{20,16},{24,20},{28,24},{32,28}... | collective-permute-start | bytes 1966088 | tf_op jit(solution)/shard_map/ppermute | solution.py:145
  78.9 13.4 %collective-permute-start.14 = (f32[8,40,512]{2,1,0:T(8,128)S(1)}, f32[8,40,512]{2,1,0:T(8,128)S(1)}, u32[]{:S(2)}, u32[]{:S(2)}) collective-permute-start(f32[8,40,512]{2,1,0:T(8,128)S(1)} %select_dynamic-update-slice_fusion.2.refs_4_), channel_id=1, source_target_pairs={{0,4},{4,8},{8,12},{12,16},{16,20},{20,24},{24,28},{28,32},{32,36}... | collective-permute-start | bytes 1966088 | tf_op jit(solution)/shard_map/ppermute | solution.py:145
  82.7 37.0 %collective-permute-start.5 = (f32[8,80,512]{2,1,0:T(8,128)S(1)}, f32[8,80,512]{2,1,0:T(8,128)S(1)}, u32[]{:S(2)}, u32[]{:S(2)}) collective-permute-start(f32[8,80,512]{2,1,0:T(8,128)S(1)} %sweep.9.refs_1_), channel_id=1, source_target_pairs={{0,252},{4,0},{8,4},{12,8},{16,12},{20,16},{24,20},{28,24},{32,28}... | collective-permute-start | bytes 3932168 | tf_op jit(solution)/shard_map/ppermute | solution.py:145
  87.5 32.2 %collective-permute-start.4 = (f32[8,80,512]{2,1,0:T(8,128)S(1)}, f32[8,80,512]{2,1,0:T(8,128)S(1)}, u32[]{:S(2)}, u32[]{:S(2)}) collective-permute-start(f32[8,80,512]{2,1,0:T(8,128)S(1)} %sweep.9.refs_1_), channel_id=1, source_target_pairs={{0,4},{4,8},{8,12},{12,16},{16,20},{20,24},{24,28},{28,32},{32,36}... | collective-permute-start | bytes 3932168 | tf_op jit(solution)/shard_map/ppermute | solution.py:145
  95.0 5.8 %collective-permute-start.16 = (f32[8,8,512]{2,1,0:T(8,128)S(1)}, f32[8,8,512]{2,1,0:T(8,128)S(1)}, u32[]{:S(2)}, u32[]{:S(2)}) collective-permute-start(f32[8,8,512]{2,1,0:T(8,128)S(1)} %get-tuple-element.18), channel_id=1, source_target_pairs={{0,3},{1,0},{2,1},{3,2},{4,7},{5,4},{6,5},{7,6},{8,11},{9,8},{10,9... | collective-permute-start | bytes 393224 | tf_op jit(solution)/shard_map/ppermute | solution.py:145
  98.3 5.0 %collective-permute-start.17 = (f32[8,8,512]{2,1,0:T(8,128)S(1)}, f32[8,8,512]{2,1,0:T(8,128)S(1)}, u32[]{:S(2)}, u32[]{:S(2)}) collective-permute-start(f32[8,8,512]{2,1,0:T(8,128)S(1)} %get-tuple-element.19), channel_id=1, source_target_pairs={{0,1},{1,2},{2,3},{3,0},{4,5},{5,6},{6,7},{7,4},{8,9},{9,10},{10,1... | collective-permute-start | bytes 393224 | tf_op jit(solution)/shard_map/ppermute | solution.py:145
  103.4 11.0 %collective-permute-start.19 = (f32[8,56,512]{2,1,0:T(8,128)S(1)}, f32[8,56,512]{2,1,0:T(8,128)S(1)}, u32[]{:S(2)}, u32[]{:S(2)}) collective-permute-start(f32[8,56,512]{2,1,0:T(8,128)S(1)} %select_dynamic-update-slice_fusion.1.refs_4_), channel_id=1, source_target_pairs={{0,252},{4,0},{8,4},{12,8},{16,12},{20,16},{24,20},{28,24},{32,28}... | collective-permute-start | bytes 2752520 | tf_op jit(solution)/shard_map/ppermute | solution.py:145
  103.5 16.2 %collective-permute-start.18 = (f32[8,56,512]{2,1,0:T(8,128)S(1)}, f32[8,56,512]{2,1,0:T(8,128)S(1)}, u32[]{:S(2)}, u32[]{:S(2)}) collective-permute-start(f32[8,56,512]{2,1,0:T(8,128)S(1)} %select_dynamic-update-slice_fusion.1.refs_4_), channel_id=1, source_target_pairs={{0,4},{4,8},{8,12},{12,16},{16,20},{20,24},{24,28},{28,32},{32,36}... | collective-permute-start | bytes 2752520 | tf_op jit(solution)/shard_map/ppermute | solution.py:145
  122.8 5.0 %collective-permute-start.20 = (f32[8,8,512]{2,1,0:T(8,128)S(1)}, f32[8,8,512]{2,1,0:T(8,128)S(1)}, u32[]{:S(2)}, u32[]{:S(2)}) collective-permute-start(f32[8,8,512]{2,1,0:T(8,128)S(1)} %get-tuple-element.21), channel_id=1, source_target_pairs={{0,3},{1,0},{2,1},{3,2},{4,7},{5,4},{6,5},{7,6},{8,11},{9,8},{10,9... | collective-permute-start | bytes 393224 | tf_op jit(solution)/shard_map/ppermute | solution.py:145
  124.2 5.0 %collective-permute-start.21 = (f32[8,8,512]{2,1,0:T(8,128)S(1)}, f32[8,8,512]{2,1,0:T(8,128)S(1)}, u32[]{:S(2)}, u32[]{:S(2)}) collective-permute-start(f32[8,8,512]{2,1,0:T(8,128)S(1)} %get-tuple-element.22), channel_id=1, source_target_pairs={{0,1},{1,2},{2,3},{3,0},{4,5},{5,6},{6,7},{7,4},{8,9},{9,10},{10,1... | collective-permute-start | bytes 393224 | tf_op jit(solution)/shard_map/ppermute | solution.py:145
  129.2 32.8 %collective-permute-start.23 = (f32[8,72,512]{2,1,0:T(8,128)S(1)}, f32[8,72,512]{2,1,0:T(8,128)S(1)}, u32[]{:S(2)}, u32[]{:S(2)}) collective-permute-start(f32[8,72,512]{2,1,0:T(8,128)S(1)} %select_dynamic-update-slice_fusion.refs_4_), channel_id=1, source_target_pairs={{0,252},{4,0},{8,4},{12,8},{16,12},{20,16},{24,20},{28,24},{32,28}... | collective-permute-start | bytes 3538952 | tf_op jit(solution)/shard_map/ppermute | solution.py:145
  129.3 32.8 %collective-permute-start.22 = (f32[8,72,512]{2,1,0:T(8,128)S(1)}, f32[8,72,512]{2,1,0:T(8,128)S(1)}, u32[]{:S(2)}, u32[]{:S(2)}) collective-permute-start(f32[8,72,512]{2,1,0:T(8,128)S(1)} %select_dynamic-update-slice_fusion.refs_4_), channel_id=1, source_target_pairs={{0,4},{4,8},{8,12},{12,16},{16,20},{20,24},{24,28},{28,32},{32,36}... | collective-permute-start | bytes 3538952 | tf_op jit(solution)/shard_map/ppermute | solution.py:145
  132.8 21.5 %collective-permute-start.7 = (f32[8,64,512]{2,1,0:T(8,128)S(1)}, f32[8,64,512]{2,1,0:T(8,128)S(1)}, u32[]{:S(2)}, u32[]{:S(2)}) collective-permute-start(f32[8,64,512]{2,1,0:T(8,128)S(1)} %sweep.10.refs_1_), channel_id=1, source_target_pairs={{0,252},{4,0},{8,4},{12,8},{16,12},{20,16},{24,20},{28,24},{32,28}... | collective-permute-start | bytes 3145736 | tf_op jit(solution)/shard_map/ppermute | solution.py:145
  137.5 22.1 %collective-permute-start.6 = (f32[8,64,512]{2,1,0:T(8,128)S(1)}, f32[8,64,512]{2,1,0:T(8,128)S(1)}, u32[]{:S(2)}, u32[]{:S(2)}) collective-permute-start(f32[8,64,512]{2,1,0:T(8,128)S(1)} %sweep.10.refs_1_), channel_id=1, source_target_pairs={{0,4},{4,8},{8,12},{12,16},{16,20},{20,24},{24,28},{28,32},{32,36}... | collective-permute-start | bytes 3145736 | tf_op jit(solution)/shard_map/ppermute | solution.py:145
  (3 other events, 38.8 us)

commit v3 on v2

--- a/solution.py
+++ b/solution.py
@@ -9,7 +9,7 @@
 REACH = 8
 LANES = 128
 TILE = 8
-MARGIN = 8
+MARGIN = 16
 
 
 def cubic_weights(shares):
@@ -26,7 +26,7 @@
     return jnp.concatenate(parts, axis=1).reshape(-1)
 
 
-def sweep(step, pieces, moves, tiles, targets, tags, table, ends=(), finish=None):
+def sweep(step, pieces, moves, tiles, targets, tags, table, ends=(), rim=None, finish=None):
     planes, _, width = pieces[0][1].shape
     blocks = width // LANES
     inputs = [part for piece in pieces for part in piece]
@@ -38,7 +38,7 @@
     def body(tag_ref, tab_ref, *refs):
         sources = refs[: len(inputs)]
         outputs = refs[len(inputs) : len(inputs) + 1 + len(ends)]
-        win, line, *more = refs[len(inputs) + 1 + len(ends) :]
+        win, line, brim, *more = refs[len(inputs) + 1 + len(ends) :]
         out_ref = outputs[0]
         if finish:
             out_ref, sems = more
@@ -53,10 +53,13 @@
                 for i, (row, height) in enumerate([(0, first), (after, whole - after)])
             ]
 
+        odd = tag_ref[6, 0]
+        starts = [planes, 2 * planes * (1 - odd), 2 * planes * odd]
+
         def fill(p, carry):
             for piece, row, at, height in moves:
                 for part in range(3):
-                    win[part * planes + p, pl.ds(at, height), :] = sources[3 * piece + part][p, pl.ds(row, height), :]
+                    win[starts[part] + p, pl.ds(at, height), :] = sources[3 * piece + part][p, pl.ds(row, height), :]
             return carry
 
         lax.fori_loop(0, planes, fill, 0)
@@ -66,39 +69,60 @@
         last_one = lane >= LANES - 1
         first_one = lane == 0
 
+        from_below = lax.broadcasted_iota(jnp.int32, (TILE, LANES), 0) < TILE // 2
+
+        def chosen(k, b, kind):
+            tag = (step * planes + k) * blocks + b
+            entry = tag_ref[2 * kind + 1, tag] * 12
+            weights = [[tab_ref[entry + 4 * axis + n] for n in range(4)] for axis in range(3)]
+            return k - tag_ref[2 * kind, tag] + (REACH - 2), weights
+
+        def along_y(base, cz, cy, b, t):
+            rows = pl.ds(t * TILE, TILE)
+            here = pl.ds(b * LANES, LANES)
+            left = pl.ds(((b - 1) % blocks) * LANES, LANES)
+            right = pl.ds(((b + 1) % blocks) * LANES, LANES)
+            mid = None
+            edge = None
+            for n in range(4):
+                m = cz[n] * win[base + n, rows, here]
+                e = cz[n] * jnp.where(from_right, win[base + n, rows, right], win[base + n, rows, left])
+                mid = m if mid is None else mid + m
+                edge = e if edge is None else edge + e
+            y = cy[2] * mid
+            y = y + cy[0] * pltpu.roll(jnp.where(last_two, edge, mid), 2, 1)
+            y = y + cy[1] * pltpu.roll(jnp.where(last_one, edge, mid), 1, 1)
+            return y + cy[3] * pltpu.roll(jnp.where(first_one, edge, mid), LANES - 1, 1)
+
+        def along_x(lines, cx, b, row):
+            acc = cx[0] * lines[b, pl.ds(row - 2, TILE), :]
+            for n in range(1, 4):
+                acc = acc + cx[n] * lines[b, pl.ds(row - 2 + n, TILE), :]
+            return acc
+
         def plane(k, carry):
             for b in range(blocks):
                 here = pl.ds(b * LANES, LANES)
-                left = pl.ds(((b - 1) % blocks) * LANES, LANES)
-                right = pl.ds(((b + 1) % blocks) * LANES, LANES)
-                tag = (step * planes + k) * blocks + b
-                base = k - tag_ref[0, tag] + (REACH - 2)
-                entry = tag_ref[1, tag] * 12
-                cz = [tab_ref[entry + n] for n in range(4)]
-                cx = [tab_ref[entry + 4 + n] for n in range(4)]
-                cy = [tab_ref[entry + 8 + n] for n in range(4)]
+                base, (cz, cx, cy) = chosen(k, b, 0)
                 for t in range(tiles):
-                    rows = pl.ds(t * TILE, TILE)
-                    mid = None
-                    edge = None
-                    for n in range(4):
-                        m = cz[n] * win[base + n, rows, here]
-                        e = cz[n] * jnp.where(from_right, win[base + n, rows, right], win[base + n, rows, left])
-                        mid = m if mid is None else mid + m
-                        edge = e if edge is None else edge + e
-                    y = cy[2] * mid
-                    y = y + cy[0] * pltpu.roll(jnp.where(last_two, edge, mid), 2, 1)
-                    y = y + cy[1] * pltpu.roll(jnp.where(last_one, edge, mid), 1, 1)
-                    y = y + cy[3] * pltpu.roll(jnp.where(first_one, edge, mid), LANES - 1, 1)
-                    line[b, rows, :] = y
+                    line[b, pl.ds(t * TILE, TILE), :] = along_y(base, cz, cy, b, t)
                 for t, row in targets:
-                    acc = cx[0] * line[b, pl.ds(t * TILE - 2, TILE), :]
-                    for n in range(1, 4):
-                        acc = acc + cx[n] * line[b, pl.ds(t * TILE - 2 + n, TILE), :]
+                    acc = along_x(line, cx, b, t * TILE)
                     out_ref[k, pl.ds(row, TILE), here] = acc
                     for end, end_ref in zip(ends, outputs[1:]):
                         if t == end:
                             end_ref[k, :, here] = acc
+                if rim:
+                    t, row = rim
+                    base, (cz, below_x, cy) = chosen(k, b, 2)
+                    for place, tile in [(0, t - 1), (TILE, t)]:
+                        brim[b, pl.ds(place, TILE), :] = along_y(base, cz, cy, b, tile)
+                    base, (cz, above_x, cy) = chosen(k, b, 1)
+                    for place, tile in [(2 * TILE, t), (3 * TILE, t + 1)]:
+                        brim[b, pl.ds(place, TILE), :] = along_y(base, cz, cy, b, tile)
+                    out_ref[k, pl.ds(row, TILE), here] = jnp.where(
+                        from_below, along_x(brim, below_x, b, TILE), along_x(brim, above_x, b, 2 * TILE)
+                    )
             if finish:
                 for copy in drains(k):
                     copy.start()
@@ -116,6 +140,7 @@
     scratch = [
         pltpu.VMEM((3 * planes, tiles * TILE, width), jnp.float32),
         pltpu.VMEM((blocks, tiles * TILE, LANES), jnp.float32),
+        pltpu.VMEM((blocks, 4 * TILE, LANES), jnp.float32),
     ]
     if finish:
         out_shape = jax.ShapeDtypeStruct((planes, whole, width), jnp.float32)
@@ -140,39 +165,50 @@
     )(tags, table, *inputs)
 
 
-def shifted(x, axis, by):
+def swapped(x, axis, first):
     devices = lax.axis_size(axis)
-    return lax.ppermute(x, axis, [(i, (i + by) % devices) for i in range(devices)])
+    pairs = []
+    for i in range(first, devices + first, 2):
+        a, b = i % devices, (i + 1) % devices
+        pairs += [(a, b), (b, a)]
+    return lax.ppermute(x, axis, pairs)
 
 
 def stacked(x):
-    up = shifted(x, "gz", 1)
-    down = shifted(x, "gz", -1)
-    return up, x, down
+    far = swapped(x, "gz", 1)
+    near = swapped(x, "gz", 0)
+    return x, near, far
 
 
 def rim_of(first, last):
-    above = shifted(last, "xy", 1)
-    below = shifted(first, "xy", -1)
-    row = lax.broadcasted_iota(jnp.int32, above.shape, 1)
-    return jnp.where(row < TILE // 2, below, above)
+    even = lax.axis_index("xy") % 2 == 0
+    one = swapped(jnp.where(even, last, first), "xy", 0)
+    other = swapped(jnp.where(even, first, last), "xy", 1)
+    row = lax.broadcasted_iota(jnp.int32, first.shape, 1)
+    return jnp.where((row < TILE // 2) == even, one, other)
 
 
 def advance(image, offsets, frac_index, fractions):
     rows = image.shape[1]
     steps = offsets.shape[0]
     table = weight_table(fractions)
+    odd = lax.axis_index("gz").astype(jnp.int32) % 2
     tags = jnp.stack([offsets.reshape(-1), frac_index.reshape(-1)])
+    even = lax.axis_index("xy") % 2 == 0
+    one, other = swapped(tags, "xy", 0), swapped(tags, "xy", 1)
+    above, below = jnp.where(even, other, one), jnp.where(even, one, other)
+    tags = jnp.concatenate([tags, above, below, jnp.full((1, offsets.size), odd)])
     margin = MARGIN
     centre = image[:, margin : rows - margin]
     first, last = image[:, :TILE], image[:, rows - TILE :]
     outer = None
     for step in range(steps):
-        rim = rim_of(first, last)
-        if outer is None:
-            outer = jnp.concatenate([image[:, rows - margin :], rim, image[:, :margin]], axis=1)
-        else:
-            outer = lax.dynamic_update_slice(outer, rim, (0, margin, 0))
+        if step % 2 == 0:
+            rim = rim_of(first, last)
+            if outer is None:
+                outer = jnp.concatenate([image[:, rows - margin :], rim, image[:, :margin]], axis=1)
+            else:
+                outer = lax.dynamic_update_slice(outer, rim, (0, margin, 0))
         inner = stacked(centre)
         outside = stacked(outer)
         tall = rows - 2 * margin
@@ -185,11 +221,14 @@
         moves = [(0, tall - 16, 0, 16), (1, 0, 16, 2 * margin - TILE), (0, 0, 8 + 2 * margin, 16)]
         upper, lower = range(1, many + 2), range(many + 3, 2 * many + 4)
         if step < steps - 1:
-            outer, last, first = sweep(
+            trade = step % 2 == 1
+            outer, *edges = sweep(
                 step, [inner, outside], moves, 2 * many + 5,
                 [(t, (t - 1) * TILE) for t in (*upper, *lower)], tags, table,
-                ends=(many + 1, many + 3),
+                ends=(many + 1, many + 3) if trade else (), rim=None if trade else (many + 2, margin),
             )
+            if trade:
+                last, first = edges
         else:
             targets = [(t, rows - margin + (t - 1) * TILE) for t in upper]
             targets += [(t, (t - many - 3) * TILE) for t in lower]

time: 167 us -> 145 us (0.87)
  waiting for transfers between devices: 100 us -> 74.5 us
  other arithmetic: 0.38 us -> 2.1 us
    ppermute x24 -> x22, waiting for transfers between devices: 100 us -> 74.5 us  [swapped(): return lax.ppermute(x, axis, pairs)]
    ppermute x24 -> x22, starting transfers between devices: 33.9 us -> 34.5 us  [swapped(): return lax.ppermute(x, axis, pairs)]
  transfers between devices with their start and end apart: 24 -> 22, of which waited for: 15 -> 9; matrix products, arithmetic and copies ran while one was open for 1% -> 3% of each run, Pallas kernels for 12% -> 12%
where the time goes in v3:
time: 145 us; the launch traced here: 144 us
  waiting for transfers between devices  74.5 us (51%)
  starting transfers between devices  34.5 us (24%)
  Pallas kernels  29.5 us (20%)
  local copies, waits for them, and re-layouts  3.35 us (2%)
  other arithmetic  2.1 us (1%)
    ppermute x22, waiting for transfers between devices, swapped(): return lax.ppermute(x, axis, pairs)  74.5 us
    ppermute x22, starting transfers between devices, swapped(): return lax.ppermute(x, axis, pairs)  34.5 us
    pallas_call x8, Pallas kernels, sweep(): pl.pallas_call(body, out_shape=out_shape, in_specs=[scalars] * 2 + [insid...  29.5 us
  transfers between devices with their start and end apart: 22, of which 9 were waited for; matrix products, arithmetic and copies ran while one was open for 3% of the time, Pallas kernels for 12%

profile of v3, /device:TPU:2, one launch (start us, length us, event | category | flops | bytes accessed | tf_op | source)
XLA Modules:
  0.0 144.4 jit_solution(8890221111626090089)
XLA Ops:
  0.0 1.6 %slice.27.refs_0_ = f32[8,96,512]{2,1,0:T(8,128)S(1)} slice(f32[8,128,512]{2,1,0:T(8,128)} %param.4), slice={[0:8], [16:112], [0:512]} | slice | bytes 3145728 | tf_op jit(solution)/shard_map/slice | solution.py:202
  1.6 7.8 %collective-permute-start.3 = (f32[8,96,512]{2,1,0:T(8,128)S(1)}, f32[8,96,512]{2,1,0:T(8,128)S(1)}, u32[]{:S(2)}, u32[]{:S(2)}) collective-permute-start(f32[8,96,512]{2,1,0:T(8,128)S(1)} %slice.27.refs_0_), channel_id=1, source_target_pairs={{4,8},{8,4},{12,16},{16,12},{20,24},{24,20},{28,32},{32,28},{36,40... | collective-permute-start | bytes 4718600 | tf_op jit(solution)/shard_map/ppermute | solution.py:174
  11.5 2.2 %collective-permute-start.11 = (f32[8,8,512]{2,1,0:T(8,128)S(1)}, f32[8,8,512]{2,1,0:T(8,128)S(1)}, u32[]{:S(2)}, u32[]{:S(2)}) collective-permute-start(f32[8,8,512]{2,1,0:T(8,128)S(1)} %get-tuple-element.13), channel_id=1, source_target_pairs={{1,2},{2,1},{3,0},{0,3},{5,6},{6,5},{7,4},{4,7},{9,10},{10,9},{11,... | collective-permute-start | bytes 393224 | tf_op jit(solution)/shard_map/ppermute | solution.py:174
  20.9 3.0 %collective-permute-done = s32[2,128]{1,0:T(2,128)S(1)} collective-permute-done((s32[2,128]{1,0:T(2,128)S(1)}, s32[2,128]{1,0:T(2,128)S(1)}, u32[]{:S(2)}, u32[]{:S(2)}) %collective-permute-start) | collective-permute-done | bytes 1056 | tf_op jit(solution)/shard_map/ppermute | solution.py:174
  23.8 3.7 %collective-permute-done.3.refs_2_ = f32[8,96,512]{2,1,0:T(8,128)S(1)} collective-permute-done((f32[8,96,512]{2,1,0:T(8,128)S(1)}, f32[8,96,512]{2,1,0:T(8,128)S(1)}, u32[]{:S(2)}, u32[]{:S(2)}) %collective-permute-start.3) | collective-permute-done | bytes 1572896 | tf_op jit(solution)/shard_map/ppermute | solution.py:174
  27.6 4.2 %sweep.8.refs_0_ = f32[8,80,512]{2,1,0:T(8,128)S(1)} custom-call(s32[7,128]{1,0:T(8,128)S(1)} %concatenate.10.tag_ref, f32[192]{0:T(256)S(1)} %reshape.3.tab_ref, f32[8,96,512]{2,1,0:T(8,128)S(1)} %slice.27.refs_0_, f32[8,96,512]{2,1,0:T(8,128)} %collective-permute-done.2.refs_1_, f32[8,96,512]{2,1,0:T(8,128)S(1)} %collective-permute-done.3.refs_2_), custom_call_target="tpu_custom_call" | custom-call | tf_op jit(solution)/shard_map/sweep/pallas_call | solution.py:157
  31.8 5.1 %collective-permute-start.5 = (f32[8,80,512]{2,1,0:T(8,128)S(1)}, f32[8,80,512]{2,1,0:T(8,128)S(1)}, u32[]{:S(2)}, u32[]{:S(2)}) collective-permute-start(f32[8,80,512]{2,1,0:T(8,128)S(1)} %sweep.8.refs_0_), channel_id=1, source_target_pairs={{4,8},{8,4},{12,16},{16,12},{20,24},{24,20},{28,32},{32,28},{36,40... | collective-permute-start | bytes 3932168 | tf_op jit(solution)/shard_map/ppermute | solution.py:174
  36.9 4.9 %sweep.11.refs_3_ = f32[8,56,512]{2,1,0:T(8,128)S(1)} custom-call(s32[7,128]{1,0:T(8,128)S(1)} %concatenate.10.tag_ref, f32[192]{0:T(256)S(1)} %reshape.3.tab_ref, f32[8,96,512]{2,1,0:T(8,128)S(1)} %slice.27.refs_0_, f32[8,96,512]{2,1,0:T(8,128)} %collective-permute-done.2.refs_1_, f32[8,96,512]{2,1,0:T(8,128)S(1)} %collective-permute-done.3.refs_2_, ...), custom_call_target="tpu_custom_call" | custom-call | tf_op jit(solution)/shard_map/sweep/pallas_call | solution.py:157
  41.9 2.9 %collective-permute-start.15 = (f32[8,56,512]{2,1,0:T(8,128)S(1)}, f32[8,56,512]{2,1,0:T(8,128)S(1)}, u32[]{:S(2)}, u32[]{:S(2)}) collective-permute-start(f32[8,56,512]{2,1,0:T(8,128)S(1)} %sweep.11.refs_3_), channel_id=1, source_target_pairs={{4,8},{8,4},{12,16},{16,12},{20,24},{24,20},{28,32},{32,28},{36,40... | collective-permute-start | bytes 2752520 | tf_op jit(solution)/shard_map/ppermute | solution.py:174
  44.8 17.3 %collective-permute-done.15.refs_5_ = f32[8,56,512]{2,1,0:T(8,128)S(1)} collective-permute-done((f32[8,56,512]{2,1,0:T(8,128)S(1)}, f32[8,56,512]{2,1,0:T(8,128)S(1)}, u32[]{:S(2)}, u32[]{:S(2)}) %collective-permute-start.15) | collective-permute-done | bytes 917536 | tf_op jit(solution)/shard_map/ppermute | solution.py:174
  62.1 3.3 %sweep.12 = (f32[8,72,512]{2,1,0:T(8,128)S(1)}, f32[8,8,512]{2,1,0:T(8,128)S(1)}, f32[8,8,512]{2,1,0:T(8,128)S(1)}) custom-call(s32[7,128]{1,0:T(8,128)S(1)} %concatenate.10.tag_ref, f32[192]{0:T(256)S(1)} %reshape.3.tab_ref, f32[8,80,512]{2,1,0:T(8,128)S(1)} %sweep.8.refs_0_, f32[8,80,512]{2,1,0:T(8,128)S(1)} %collective-permute-done.4.refs_1_, ...), custom_call_target="tpu_custom_call" | custom-call | tf_op jit(solution)/shard_map/sweep/pallas_call | solution.py:157
  65.4 1.6 %collective-permute-start.17 = (f32[8,8,512]{2,1,0:T(8,128)S(1)}, f32[8,8,512]{2,1,0:T(8,128)S(1)}, u32[]{:S(2)}, u32[]{:S(2)}) collective-permute-start(f32[8,8,512]{2,1,0:T(8,128)S(1)} %get-tuple-element.15), channel_id=1, source_target_pairs={{1,2},{2,1},{3,0},{0,3},{5,6},{6,5},{7,4},{4,7},{9,10},{10,9},{11,... | collective-permute-start | bytes 393224 | tf_op jit(solution)/shard_map/ppermute | solution.py:174
  67.0 1.8 %collective-permute-start.16 = (f32[8,8,512]{2,1,0:T(8,128)S(1)}, f32[8,8,512]{2,1,0:T(8,128)S(1)}, u32[]{:S(2)}, u32[]{:S(2)}) collective-permute-start(f32[8,8,512]{2,1,0:T(8,128)S(1)} %get-tuple-element.16), channel_id=1, source_target_pairs={{0,1},{1,0},{2,3},{3,2},{4,5},{5,4},{6,7},{7,6},{8,9},{9,8},{10,11... | collective-permute-start | bytes 393224 | tf_op jit(solution)/shard_map/ppermute | solution.py:174
  68.8 1.7 %collective-permute-done.17 = f32[8,8,512]{2,1,0:T(8,128)S(1)} collective-permute-done((f32[8,8,512]{2,1,0:T(8,128)S(1)}, f32[8,8,512]{2,1,0:T(8,128)S(1)}, u32[]{:S(2)}, u32[]{:S(2)}) %collective-permute-start.17) | collective-permute-done | bytes 131104 | tf_op jit(solution)/shard_map/ppermute | solution.py:174
  70.4 1.5 %collective-permute-done.16 = f32[8,8,512]{2,1,0:T(8,128)S(1)} collective-permute-done((f32[8,8,512]{2,1,0:T(8,128)S(1)}, f32[8,8,512]{2,1,0:T(8,128)S(1)}, u32[]{:S(2)}, u32[]{:S(2)}) %collective-permute-start.16) | collective-permute-done | bytes 131104 | tf_op jit(solution)/shard_map/ppermute | solution.py:174
  72.0 4.1 %collective-permute-start.19 = (f32[8,72,512]{2,1,0:T(8,128)S(1)}, f32[8,72,512]{2,1,0:T(8,128)S(1)}, u32[]{:S(2)}, u32[]{:S(2)}) collective-permute-start(f32[8,72,512]{2,1,0:T(8,128)S(1)} %select_dynamic-update-slice_fusion.refs_3_), channel_id=1, source_target_pairs={{4,8},{8,4},{12,16},{16,12},{20,24},{24,20},{28,32},{32,28},{36,40... | collective-permute-start | bytes 3538952 | tf_op jit(solution)/shard_map/ppermute | solution.py:174
  76.1 3.0 %sweep.9.refs_0_ = f32[8,64,512]{2,1,0:T(8,128)S(1)} custom-call(s32[7,128]{1,0:T(8,128)S(1)} %concatenate.10.tag_ref, f32[192]{0:T(256)S(1)} %reshape.3.tab_ref, f32[8,80,512]{2,1,0:T(8,128)S(1)} %sweep.8.refs_0_, f32[8,80,512]{2,1,0:T(8,128)S(1)} %collective-permute-done.4.refs_1_, f32[8,80,512]{2,1,0:T(8,128)S(1)} %collective-permute-done.5.refs_2_), custom_call_target="tpu_custom_call" | custom-call | tf_op jit(solution)/shard_map/sweep/pallas_call | solution.py:157
  80.3 22.0 %collective-permute-done.7.refs_2_ = f32[8,64,512]{2,1,0:T(8,128)S(1)} collective-permute-done((f32[8,64,512]{2,1,0:T(8,128)S(1)}, f32[8,64,512]{2,1,0:T(8,128)S(1)}, u32[]{:S(2)}, u32[]{:S(2)}) %collective-permute-start.7) | collective-permute-done | bytes 1048608 | tf_op jit(solution)/shard_map/ppermute | solution.py:174
  102.3 4.4 %sweep.13.refs_3_ = f32[8,88,512]{2,1,0:T(8,128)S(1)} custom-call(s32[7,128]{1,0:T(8,128)S(1)} %concatenate.10.tag_ref, f32[192]{0:T(256)S(1)} %reshape.3.tab_ref, f32[8,64,512]{2,1,0:T(8,128)S(1)} %sweep.9.refs_0_, f32[8,64,512]{2,1,0:T(8,128)S(1)} %collective-permute-done.6.refs_1_, f32[8,64,512]{2,1,0:T(8,128)S(1)} %collective-permute-done.7.refs_2_, ...), custom_call_target="tpu_custom_call" | custom-call | tf_op jit(solution)/shard_map/sweep/pallas_call | solution.py:157
  106.7 4.1 %collective-permute-start.21 = (f32[8,88,512]{2,1,0:T(8,128)S(1)}, f32[8,88,512]{2,1,0:T(8,128)S(1)}, u32[]{:S(2)}, u32[]{:S(2)}) collective-permute-start(f32[8,88,512]{2,1,0:T(8,128)S(1)} %sweep.13.refs_3_), channel_id=1, source_target_pairs={{4,8},{8,4},{12,16},{16,12},{20,24},{24,20},{28,32},{32,28},{36,40... | collective-permute-start | bytes 4325384 | tf_op jit(solution)/shard_map/ppermute | solution.py:174
  110.8 2.5 %sweep.10.refs_0_ = f32[8,48,512]{2,1,0:T(8,128)S(1)} custom-call(s32[7,128]{1,0:T(8,128)S(1)} %concatenate.10.tag_ref, f32[192]{0:T(256)S(1)} %reshape.3.tab_ref, f32[8,64,512]{2,1,0:T(8,128)S(1)} %sweep.9.refs_0_, f32[8,64,512]{2,1,0:T(8,128)S(1)} %collective-permute-done.6.refs_1_, f32[8,64,512]{2,1,0:T(8,128)S(1)} %collective-permute-done.7.refs_2_), custom_call_target="tpu_custom_call" | custom-call | tf_op jit(solution)/shard_map/sweep/pallas_call | solution.py:157
  114.5 22.5 %collective-permute-done.9.refs_2_ = f32[8,48,512]{2,1,0:T(8,128)S(1)} collective-permute-done((f32[8,48,512]{2,1,0:T(8,128)S(1)}, f32[8,48,512]{2,1,0:T(8,128)S(1)}, u32[]{:S(2)}, u32[]{:S(2)}) %collective-permute-start.9) | collective-permute-done | bytes 786464 | tf_op jit(solution)/shard_map/ppermute | solution.py:174
  137.0 2.3 %sweep.14.refs_6_ = f32[8,32,512]{2,1,0:T(8,128)S(1)} custom-call(s32[7,128]{1,0:T(8,128)S(1)} %concatenate.10.tag_ref, f32[192]{0:T(256)S(1)} %reshape.3.tab_ref, f32[8,48,512]{2,1,0:T(8,128)S(1)} %sweep.10.refs_0_, f32[8,48,512]{2,1,0:T(8,128)S(1)} %collective-permute-done.8.refs_1_, f32[8,48,512]{2,1,0:T(8,128)S(1)} %collective-permute-done.9.refs_2_), custom_call_target="tpu_custom_call" | custom-call | tf_op jit(solution)/shard_map/sweep/pallas_call | solution.py:157
  139.3 4.9 %sweep.15 = f32[8,128,512]{2,1,0:T(8,128)} custom-call(s32[7,128]{1,0:T(8,128)S(1)} %concatenate.10.tag_ref, f32[192]{0:T(256)S(1)} %reshape.3.tab_ref, f32[8,48,512]{2,1,0:T(8,128)S(1)} %sweep.10.refs_0_, f32[8,48,512]{2,1,0:T(8,128)S(1)} %collective-permute-done.8.refs_1_, f32[8,48,512]{2,1,0:T(8,128)S(1)} %collective-permute-done.9.refs_2_, ...), custom_call_target="tpu_custom_call" | custom-call | tf_op jit(solution)/shard_map/sweep/pallas_call | solution.py:157
  (54 shorter events, 11.6 us)
Async XLA Ops:
  0.0 9.5 %copy-start = (s32[4,8,1,4]{1,3,2,0:T(4,128)S(1)}, s32[4,8,1,4]{1,3,2,0:T(4,128)}, u32[]{:S(2)}) copy-start(s32[4,8,1,4]{1,3,2,0:T(4,128)} %param.5) | copy-start | bytes 1540
  0.0 9.7 %copy-start.1 = (s32[4,8,1,4]{1,3,2,0:T(4,128)S(1)}, s32[4,8,1,4]{1,3,2,0:T(4,128)}, u32[]{:S(2)}) copy-start(s32[4,8,1,4]{1,3,2,0:T(4,128)} %param.6) | copy-start | bytes 1540
  1.6 25.9 %collective-permute-start.3 = (f32[8,96,512]{2,1,0:T(8,128)S(1)}, f32[8,96,512]{2,1,0:T(8,128)S(1)}, u32[]{:S(2)}, u32[]{:S(2)}) collective-permute-start(f32[8,96,512]{2,1,0:T(8,128)S(1)} %slice.27.refs_0_), channel_id=1, source_target_pairs={{4,8},{8,4},{12,16},{16,12},{20,24},{24,20},{28,32},{32,28},{36,40... | collective-permute-start | bytes 4718600 | tf_op jit(solution)/shard_map/ppermute | solution.py:174
  9.5 18.1 %collective-permute-start.2 = (f32[8,96,512]{2,1,0:T(8,128)S(1)}, f32[8,96,512]{2,1,0:T(8,128)}, u32[]{:S(2)}, u32[]{:S(2)}) collective-permute-start(f32[8,96,512]{2,1,0:T(8,128)S(1)} %slice.27.refs_0_), channel_id=1, source_target_pairs={{0,4},{4,0},{8,12},{12,8},{16,20},{20,16},{24,28},{28,24},{32,36},... | collective-permute-start | bytes 4718600 | tf_op jit(solution)/shard_map/ppermute | solution.py:174
  9.9 10.2 %collective-permute-start.1 = (s32[2,128]{1,0:T(2,128)S(1)}, s32[2,128]{1,0:T(2,128)S(1)}, u32[]{:S(2)}, u32[]{:S(2)}) collective-permute-start(s32[2,128]{1,0:T(2,128)S(1)} %pad_add_fusion), channel_id=1, source_target_pairs={{0,1},{1,0},{2,3},{3,2},{4,5},{5,4},{6,7},{7,6},{8,9},{9,8},{10,11... | collective-permute-start | bytes 3080 | tf_op jit(solution)/shard_map/ppermute | solution.py:174
  11.5 6.1 %collective-permute-start.11 = (f32[8,8,512]{2,1,0:T(8,128)S(1)}, f32[8,8,512]{2,1,0:T(8,128)S(1)}, u32[]{:S(2)}, u32[]{:S(2)}) collective-permute-start(f32[8,8,512]{2,1,0:T(8,128)S(1)} %get-tuple-element.13), channel_id=1, source_target_pairs={{1,2},{2,1},{3,0},{0,3},{5,6},{6,5},{7,4},{4,7},{9,10},{10,9},{11,... | collective-permute-start | bytes 393224 | tf_op jit(solution)/shard_map/ppermute | solution.py:174
  13.8 5.3 %collective-permute-start.10 = (f32[8,8,512]{2,1,0:T(8,128)S(1)}, f32[8,8,512]{2,1,0:T(8,128)S(1)}, u32[]{:S(2)}, u32[]{:S(2)}) collective-permute-start(f32[8,8,512]{2,1,0:T(8,128)S(1)} %get-tuple-element.14), channel_id=1, source_target_pairs={{0,1},{1,0},{2,3},{3,2},{4,5},{5,4},{6,7},{7,6},{8,9},{9,8},{10,11... | collective-permute-start | bytes 393224 | tf_op jit(solution)/shard_map/ppermute | solution.py:174
  20.1 16.8 %collective-permute-start.13 = (f32[8,40,512]{2,1,0:T(8,128)}, f32[8,40,512]{2,1,0:T(8,128)}, u32[]{:S(2)}, u32[]{:S(2)}) collective-permute-start(f32[8,40,512]{2,1,0:T(8,128)} %pad_maximum_fusion.refs_3_), channel_id=1, source_target_pairs={{4,8},{8,4},{12,16},{16,12},{20,24},{24,20},{28,32},{32,28},{36,40... | collective-permute-start | bytes 1966088 | tf_op jit(solution)/shard_map/ppermute | solution.py:174
  20.1 16.8 %collective-permute-start.12 = (f32[8,40,512]{2,1,0:T(8,128)}, f32[8,40,512]{2,1,0:T(8,128)}, u32[]{:S(2)}, u32[]{:S(2)}) collective-permute-start(f32[8,40,512]{2,1,0:T(8,128)} %pad_maximum_fusion.refs_3_), channel_id=1, source_target_pairs={{0,4},{4,0},{8,12},{12,8},{16,20},{20,16},{24,28},{28,24},{32,36},... | collective-permute-start | bytes 1966088 | tf_op jit(solution)/shard_map/ppermute | solution.py:174
  20.2 3.7 %collective-permute-start = (s32[2,128]{1,0:T(2,128)S(1)}, s32[2,128]{1,0:T(2,128)S(1)}, u32[]{:S(2)}, u32[]{:S(2)}) collective-permute-start(s32[2,128]{1,0:T(2,128)S(1)} %pad_add_fusion), channel_id=1, source_target_pairs={{1,2},{2,1},{3,0},{0,3},{5,6},{6,5},{7,4},{4,7},{9,10},{10,9},{11,... | collective-permute-start | bytes 3080 | tf_op jit(solution)/shard_map/ppermute | solution.py:174
  31.8 30.3 %collective-permute-start.5 = (f32[8,80,512]{2,1,0:T(8,128)S(1)}, f32[8,80,512]{2,1,0:T(8,128)S(1)}, u32[]{:S(2)}, u32[]{:S(2)}) collective-permute-start(f32[8,80,512]{2,1,0:T(8,128)S(1)} %sweep.8.refs_0_), channel_id=1, source_target_pairs={{4,8},{8,4},{12,16},{16,12},{20,24},{24,20},{28,32},{32,28},{36,40... | collective-permute-start | bytes 3932168 | tf_op jit(solution)/shard_map/ppermute | solution.py:174
  36.9 25.1 %collective-permute-start.4 = (f32[8,80,512]{2,1,0:T(8,128)S(1)}, f32[8,80,512]{2,1,0:T(8,128)S(1)}, u32[]{:S(2)}, u32[]{:S(2)}) collective-permute-start(f32[8,80,512]{2,1,0:T(8,128)S(1)} %sweep.8.refs_0_), channel_id=1, source_target_pairs={{0,4},{4,0},{8,12},{12,8},{16,20},{20,16},{24,28},{28,24},{32,36},... | collective-permute-start | bytes 3932168 | tf_op jit(solution)/shard_map/ppermute | solution.py:174
  41.9 20.2 %collective-permute-start.15 = (f32[8,56,512]{2,1,0:T(8,128)S(1)}, f32[8,56,512]{2,1,0:T(8,128)S(1)}, u32[]{:S(2)}, u32[]{:S(2)}) collective-permute-start(f32[8,56,512]{2,1,0:T(8,128)S(1)} %sweep.11.refs_3_), channel_id=1, source_target_pairs={{4,8},{8,4},{12,16},{16,12},{20,24},{24,20},{28,32},{32,28},{36,40... | collective-permute-start | bytes 2752520 | tf_op jit(solution)/shard_map/ppermute | solution.py:174
  44.8 17.3 %collective-permute-start.14 = (f32[8,56,512]{2,1,0:T(8,128)S(1)}, f32[8,56,512]{2,1,0:T(8,128)S(1)}, u32[]{:S(2)}, u32[]{:S(2)}) collective-permute-start(f32[8,56,512]{2,1,0:T(8,128)S(1)} %sweep.11.refs_3_), channel_id=1, source_target_pairs={{0,4},{4,0},{8,12},{12,8},{16,20},{20,16},{24,28},{28,24},{32,36},... | collective-permute-start | bytes 2752520 | tf_op jit(solution)/shard_map/ppermute | solution.py:174
  65.4 5.1 %collective-permute-start.17 = (f32[8,8,512]{2,1,0:T(8,128)S(1)}, f32[8,8,512]{2,1,0:T(8,128)S(1)}, u32[]{:S(2)}, u32[]{:S(2)}) collective-permute-start(f32[8,8,512]{2,1,0:T(8,128)S(1)} %get-tuple-element.15), channel_id=1, source_target_pairs={{1,2},{2,1},{3,0},{0,3},{5,6},{6,5},{7,4},{4,7},{9,10},{10,9},{11,... | collective-permute-start | bytes 393224 | tf_op jit(solution)/shard_map/ppermute | solution.py:174
  67.0 5.0 %collective-permute-start.16 = (f32[8,8,512]{2,1,0:T(8,128)S(1)}, f32[8,8,512]{2,1,0:T(8,128)S(1)}, u32[]{:S(2)}, u32[]{:S(2)}) collective-permute-start(f32[8,8,512]{2,1,0:T(8,128)S(1)} %get-tuple-element.16), channel_id=1, source_target_pairs={{0,1},{1,0},{2,3},{3,2},{4,5},{5,4},{6,7},{7,6},{8,9},{9,8},{10,11... | collective-permute-start | bytes 393224 | tf_op jit(solution)/shard_map/ppermute | solution.py:174
  72.0 30.3 %collective-permute-start.19 = (f32[8,72,512]{2,1,0:T(8,128)S(1)}, f32[8,72,512]{2,1,0:T(8,128)S(1)}, u32[]{:S(2)}, u32[]{:S(2)}) collective-permute-start(f32[8,72,512]{2,1,0:T(8,128)S(1)} %select_dynamic-update-slice_fusion.refs_3_), channel_id=1, source_target_pairs={{4,8},{8,4},{12,16},{16,12},{20,24},{24,20},{28,32},{32,28},{36,40... | collective-permute-start | bytes 3538952 | tf_op jit(solution)/shard_map/ppermute | solution.py:174
  76.1 26.2 %collective-permute-start.18 = (f32[8,72,512]{2,1,0:T(8,128)S(1)}, f32[8,72,512]{2,1,0:T(8,128)S(1)}, u32[]{:S(2)}, u32[]{:S(2)}) collective-permute-start(f32[8,72,512]{2,1,0:T(8,128)S(1)} %select_dynamic-update-slice_fusion.refs_3_), channel_id=1, source_target_pairs={{0,4},{4,0},{8,12},{12,8},{16,20},{20,16},{24,28},{28,24},{32,36},... | collective-permute-start | bytes 3538952 | tf_op jit(solution)/shard_map/ppermute | solution.py:174
  79.1 23.2 %collective-permute-start.7 = (f32[8,64,512]{2,1,0:T(8,128)S(1)}, f32[8,64,512]{2,1,0:T(8,128)S(1)}, u32[]{:S(2)}, u32[]{:S(2)}) collective-permute-start(f32[8,64,512]{2,1,0:T(8,128)S(1)} %sweep.9.refs_0_), channel_id=1, source_target_pairs={{4,8},{8,4},{12,16},{16,12},{20,24},{24,20},{28,32},{32,28},{36,40... | collective-permute-start | bytes 3145736 | tf_op jit(solution)/shard_map/ppermute | solution.py:174
  80.3 22.0 %collective-permute-start.6 = (f32[8,64,512]{2,1,0:T(8,128)S(1)}, f32[8,64,512]{2,1,0:T(8,128)S(1)}, u32[]{:S(2)}, u32[]{:S(2)}) collective-permute-start(f32[8,64,512]{2,1,0:T(8,128)S(1)} %sweep.9.refs_0_), channel_id=1, source_target_pairs={{0,4},{4,0},{8,12},{12,8},{16,20},{20,16},{24,28},{28,24},{32,36},... | collective-permute-start | bytes 3145736 | tf_op jit(solution)/shard_map/ppermute | solution.py:174
  106.7 32.6 %collective-permute-start.21 = (f32[8,88,512]{2,1,0:T(8,128)S(1)}, f32[8,88,512]{2,1,0:T(8,128)S(1)}, u32[]{:S(2)}, u32[]{:S(2)}) collective-permute-start(f32[8,88,512]{2,1,0:T(8,128)S(1)} %sweep.13.refs_3_), channel_id=1, source_target_pairs={{4,8},{8,4},{12,16},{16,12},{20,24},{24,20},{28,32},{32,28},{36,40... | collective-permute-start | bytes 4325384 | tf_op jit(solution)/shard_map/ppermute | solution.py:174
  110.8 28.5 %collective-permute-start.20 = (f32[8,88,512]{2,1,0:T(8,128)S(1)}, f32[8,88,512]{2,1,0:T(8,128)S(1)}, u32[]{:S(2)}, u32[]{:S(2)}) collective-permute-start(f32[8,88,512]{2,1,0:T(8,128)S(1)} %sweep.13.refs_3_), channel_id=1, source_target_pairs={{0,4},{4,0},{8,12},{12,8},{16,20},{20,16},{24,28},{28,24},{32,36},... | collective-permute-start | bytes 4325384 | tf_op jit(solution)/shard_map/ppermute | solution.py:174
  113.3 23.7 %collective-permute-start.9 = (f32[8,48,512]{2,1,0:T(8,128)S(1)}, f32[8,48,512]{2,1,0:T(8,128)S(1)}, u32[]{:S(2)}, u32[]{:S(2)}) collective-permute-start(f32[8,48,512]{2,1,0:T(8,128)S(1)} %sweep.10.refs_0_), channel_id=1, source_target_pairs={{4,8},{8,4},{12,16},{16,12},{20,24},{24,20},{28,32},{32,28},{36,40... | collective-permute-start | bytes 2359304 | tf_op jit(solution)/shard_map/ppermute | solution.py:174
  114.5 22.5 %collective-permute-start.8 = (f32[8,48,512]{2,1,0:T(8,128)S(1)}, f32[8,48,512]{2,1,0:T(8,128)S(1)}, u32[]{:S(2)}, u32[]{:S(2)}) collective-permute-start(f32[8,48,512]{2,1,0:T(8,128)S(1)} %sweep.10.refs_0_), channel_id=1, source_target_pairs={{0,4},{4,0},{8,12},{12,8},{16,20},{20,16},{24,28},{28,24},{32,36},... | collective-permute-start | bytes 2359304 | tf_op jit(solution)/shard_map/ppermute | solution.py:174
  (1 other events, 8.6 us)

commit v4 on v3

--- a/solution.py
+++ b/solution.py
@@ -26,7 +26,7 @@
     return jnp.concatenate(parts, axis=1).reshape(-1)
 
 
-def sweep(step, pieces, moves, tiles, targets, tags, table, ends=(), rim=None, finish=None):
+def sweep(step, pieces, moves, tiles, targets, tags, table, rim=None, finish=None):
     planes, _, width = pieces[0][1].shape
     blocks = width // LANES
     inputs = [part for piece in pieces for part in piece]
@@ -37,18 +37,17 @@
 
     def body(tag_ref, tab_ref, *refs):
         sources = refs[: len(inputs)]
-        outputs = refs[len(inputs) : len(inputs) + 1 + len(ends)]
-        win, line, brim, *more = refs[len(inputs) + 1 + len(ends) :]
-        out_ref = outputs[0]
+        result, win, line, brim, *more = refs[len(inputs) :]
+        out_ref = result
         if finish:
             out_ref, sems = more
-            last = pltpu.make_async_copy(sources[-1], outputs[0].at[:, pl.ds(first, after - first), :], sems.at[0])
+            last = pltpu.make_async_copy(sources[-1], result.at[:, pl.ds(first, after - first), :], sems.at[0])
             last.start()
 
         def drains(k):
             return [
                 pltpu.make_async_copy(
-                    out_ref.at[k, pl.ds(row, height), :], outputs[0].at[k, pl.ds(row, height), :], sems.at[1 + 2 * k + i]
+                    out_ref.at[k, pl.ds(row, height), :], result.at[k, pl.ds(row, height), :], sems.at[1 + 2 * k + i]
                 )
                 for i, (row, height) in enumerate([(0, first), (after, whole - after)])
             ]
@@ -107,11 +106,7 @@
                 for t in range(tiles):
                     line[b, pl.ds(t * TILE, TILE), :] = along_y(base, cz, cy, b, t)
                 for t, row in targets:
-                    acc = along_x(line, cx, b, t * TILE)
-                    out_ref[k, pl.ds(row, TILE), here] = acc
-                    for end, end_ref in zip(ends, outputs[1:]):
-                        if t == end:
-                            end_ref[k, :, here] = acc
+                    out_ref[k, pl.ds(row, TILE), here] = along_x(line, cx, b, t * TILE)
                 if rim:
                     t, row = rim
                     base, (cz, below_x, cy) = chosen(k, b, 2)
@@ -128,7 +123,10 @@
                     copy.start()
             return carry
 
-        lax.fori_loop(0, planes, plane, 0)
+        def two_planes(i, carry):
+            return plane(2 * i + 1, plane(2 * i, carry))
+
+        lax.fori_loop(0, planes // 2, two_planes, 0)
         if finish:
             last.wait()
             for k in range(planes):
@@ -152,8 +150,7 @@
     else:
         height = max(row for _, row in targets) + TILE
         out_shape = [jax.ShapeDtypeStruct((planes, height, width), jnp.float32)]
-        out_shape += [jax.ShapeDtypeStruct((planes, TILE, width), jnp.float32)] * len(ends)
-        out_specs = [inside] * len(out_shape)
+        out_specs = [inside]
     return pl.pallas_call(
         body,
         out_shape=out_shape,
@@ -220,15 +217,18 @@
         )
         moves = [(0, tall - 16, 0, 16), (1, 0, 16, 2 * margin - TILE), (0, 0, 8 + 2 * margin, 16)]
         upper, lower = range(1, many + 2), range(many + 3, 2 * many + 4)
+        trade = step % 2 == 1 and step < steps - 1
+        if trade:
+            (ends,) = sweep(
+                step, [outside], [(0, margin - TILE - 16, 0, 40)], 5, [(1, 0), (3, TILE)], tags, table,
+            )
+            last, first = ends[:, :TILE], ends[:, TILE:]
         if step < steps - 1:
-            trade = step % 2 == 1
-            outer, *edges = sweep(
+            (outer,) = sweep(
                 step, [inner, outside], moves, 2 * many + 5,
                 [(t, (t - 1) * TILE) for t in (*upper, *lower)], tags, table,
-                ends=(many + 1, many + 3) if trade else (), rim=None if trade else (many + 2, margin),
+                rim=None if trade else (many + 2, margin),
             )
-            if trade:
-                last, first = edges
         else:
             targets = [(t, rows - margin + (t - 1) * TILE) for t in upper]
             targets += [(t, (t - many - 3) * TILE) for t in lower]

time: 145 us -> 142 us (0.979)
  the two profiles are of different devices: /device:TPU:2 before, /device:TPU:6 now
where the time goes in v4:
time: 142 us
  waiting for transfers between devices  75.7 us (53%)
  starting transfers between devices  31.9 us (22%)
  Pallas kernels  28.5 us (20%)
  local copies, waits for them, and re-layouts  3.33 us (2%)
  other arithmetic  2.1 us (1%)
    ppermute x22, waiting for transfers between devices, swapped(): return lax.ppermute(x, axis, pairs)  75.7 us
    ppermute x22, starting transfers between devices, swapped(): return lax.ppermute(x, axis, pairs)  31.9 us
    pallas_call x9, Pallas kernels, sweep(): pl.pallas_call(body, out_shape=out_shape, in_specs=[scalars] * 2 + [insid...  28.5 us
  transfers between devices with their start and end apart: 22, of which 8 were waited for; matrix products, arithmetic and copies ran while one was open for 3% of the time, Pallas kernels for 14%

profile of v4, /device:TPU:6, one launch (start us, length us, event | category | flops | bytes accessed | tf_op | source)
XLA Modules:
  0.0 142.0 jit_solution(1139180940972303734)
XLA Ops:
  1.6 7.8 %collective-permute-start.3 = (f32[8,96,512]{2,1,0:T(8,128)S(1)}, f32[8,96,512]{2,1,0:T(8,128)S(1)}, u32[]{:S(2)}, u32[]{:S(2)}) collective-permute-start(f32[8,96,512]{2,1,0:T(8,128)S(1)} %slice.33.refs_0_), channel_id=1, source_target_pairs={{4,8},{8,4},{12,16},{16,12},{20,24},{24,20},{28,32},{32,28},{36,40... | collective-permute-start | bytes 4718600 | tf_op jit(solution)/shard_map/ppermute | solution.py:171
  13.0 4.7 %collective-permute-done.11 = f32[8,8,512]{2,1,0:T(8,128)S(1)} collective-permute-done((f32[8,8,512]{2,1,0:T(8,128)S(1)}, f32[8,8,512]{2,1,0:T(8,128)S(1)}, u32[]{:S(2)}, u32[]{:S(2)}) %collective-permute-start.11) | collective-permute-done | bytes 131104 | tf_op jit(solution)/shard_map/ppermute | solution.py:171
  19.2 3.5 %collective-permute-done.1 = s32[2,128]{1,0:T(2,128)S(1)} collective-permute-done((s32[2,128]{1,0:T(2,128)S(1)}, s32[2,128]{1,0:T(2,128)S(1)}, u32[]{:S(2)}, u32[]{:S(2)}) %collective-permute-start.1) | collective-permute-done | bytes 1056 | tf_op jit(solution)/shard_map/ppermute | solution.py:171
  22.8 1.7 %collective-permute-start = (s32[2,128]{1,0:T(2,128)S(1)}, s32[2,128]{1,0:T(2,128)S(1)}, u32[]{:S(2)}, u32[]{:S(2)}) collective-permute-start(s32[2,128]{1,0:T(2,128)S(1)} %pad_add_fusion), channel_id=1, source_target_pairs={{1,2},{2,1},{3,0},{0,3},{5,6},{6,5},{7,4},{4,7},{9,10},{10,9},{11,... | collective-permute-start | bytes 3080 | tf_op jit(solution)/shard_map/ppermute | solution.py:171
  24.7 2.8 %collective-permute-done = s32[2,128]{1,0:T(2,128)S(1)} collective-permute-done((s32[2,128]{1,0:T(2,128)S(1)}, s32[2,128]{1,0:T(2,128)S(1)}, u32[]{:S(2)}, u32[]{:S(2)}) %collective-permute-start) | collective-permute-done | bytes 1056 | tf_op jit(solution)/shard_map/ppermute | solution.py:171
  27.6 4.0 %sweep.9.refs_0_ = f32[8,80,512]{2,1,0:T(8,128)S(1)} custom-call(s32[7,128]{1,0:T(8,128)S(1)} %concatenate.10.tag_ref, f32[192]{0:T(256)S(1)} %reshape.3.tab_ref, f32[8,96,512]{2,1,0:T(8,128)S(1)} %slice.33.refs_0_, f32[8,96,512]{2,1,0:T(8,128)} %collective-permute-done.2.refs_1_, f32[8,96,512]{2,1,0:T(8,128)S(1)} %collective-permute-done.3.refs_2_), custom_call_target="tpu_custom_call" | custom-call | tf_op jit(solution)/shard_map/sweep/pallas_call | solution.py:154
  31.6 5.1 %collective-permute-start.5 = (f32[8,80,512]{2,1,0:T(8,128)S(1)}, f32[8,80,512]{2,1,0:T(8,128)S(1)}, u32[]{:S(2)}, u32[]{:S(2)}) collective-permute-start(f32[8,80,512]{2,1,0:T(8,128)S(1)} %sweep.9.refs_0_), channel_id=1, source_target_pairs={{4,8},{8,4},{12,16},{16,12},{20,24},{24,20},{28,32},{32,28},{36,40... | collective-permute-start | bytes 3932168 | tf_op jit(solution)/shard_map/ppermute | solution.py:171
  36.7 4.5 %sweep.12.refs_3_.refs_0_ = f32[8,56,512]{2,1,0:T(8,128)S(1)} custom-call(s32[7,128]{1,0:T(8,128)S(1)} %concatenate.10.tag_ref, f32[192]{0:T(256)S(1)} %reshape.3.tab_ref, f32[8,96,512]{2,1,0:T(8,128)S(1)} %slice.33.refs_0_, f32[8,96,512]{2,1,0:T(8,128)} %collective-permute-done.2.refs_1_, f32[8,96,512]{2,1,0:T(8,128)S(1)} %collective-permute-done.3.refs_2_, ...), custom_call_target="tpu_custom_call" | custom-call | tf_op jit(solution)/shard_map/sweep/pallas_call | solution.py:154
  41.1 3.1 %collective-permute-start.15 = (f32[8,56,512]{2,1,0:T(8,128)S(1)}, f32[8,56,512]{2,1,0:T(8,128)S(1)}, u32[]{:S(2)}, u32[]{:S(2)}) collective-permute-start(f32[8,56,512]{2,1,0:T(8,128)S(1)} %sweep.12.refs_3_.refs_0_), channel_id=1, source_target_pairs={{4,8},{8,4},{12,16},{16,12},{20,24},{24,20},{28,32},{32,28},{36,40... | collective-permute-start | bytes 2752520 | tf_op jit(solution)/shard_map/ppermute | solution.py:171
  44.3 17.5 %collective-permute-done.15.refs_5_.refs_2_ = f32[8,56,512]{2,1,0:T(8,128)S(1)} collective-permute-done((f32[8,56,512]{2,1,0:T(8,128)S(1)}, f32[8,56,512]{2,1,0:T(8,128)S(1)}, u32[]{:S(2)}, u32[]{:S(2)}) %collective-permute-start.15) | collective-permute-done | bytes 917536 | tf_op jit(solution)/shard_map/ppermute | solution.py:171
  61.8 1.7 %sweep.14 = f32[8,16,512]{2,1,0:T(8,128)S(1)} custom-call(s32[7,128]{1,0:T(8,128)S(1)} %concatenate.10.tag_ref, f32[192]{0:T(256)S(1)} %reshape.3.tab_ref, f32[8,56,512]{2,1,0:T(8,128)S(1)} %sweep.12.refs_3_.refs_0_, f32[8,56,512]{2,1,0:T(8,128)S(1)} %collective-permute-done.14.refs_4_.refs_1_, f32[8,56,512]{2,1,0:T(8,128)S(1)} %collective-permute-done.15.refs_5_.refs_2_), custom_call_target="tpu_custom_call" | custom-call | tf_op jit(solution)/shard_map/sweep/pallas_call | solution.py:154
  63.6 1.8 %collective-permute-start.17 = (f32[8,8,512]{2,1,0:T(8,128)S(1)}, f32[8,8,512]{2,1,0:T(8,128)S(1)}, u32[]{:S(2)}, u32[]{:S(2)}) collective-permute-start(f32[8,8,512]{2,1,0:T(8,128)S(1)} %get-tuple-element.9), channel_id=1, source_target_pairs={{1,2},{2,1},{3,0},{0,3},{5,6},{6,5},{7,4},{4,7},{9,10},{10,9},{11,... | collective-permute-start | bytes 393224 | tf_op jit(solution)/shard_map/ppermute | solution.py:171
  65.4 2.9 %sweep.13 = f32[8,72,512]{2,1,0:T(8,128)S(1)} custom-call(s32[7,128]{1,0:T(8,128)S(1)} %concatenate.10.tag_ref, f32[192]{0:T(256)S(1)} %reshape.3.tab_ref, f32[8,80,512]{2,1,0:T(8,128)S(1)} %sweep.9.refs_0_, f32[8,80,512]{2,1,0:T(8,128)S(1)} %collective-permute-done.4.refs_1_, f32[8,80,512]{2,1,0:T(8,128)S(1)} %collective-permute-done.5.refs_2_, ...), custom_call_target="tpu_custom_call" | custom-call | tf_op jit(solution)/shard_map/sweep/pallas_call | solution.py:154
  70.5 3.4 %collective-permute-start.19 = (f32[8,72,512]{2,1,0:T(8,128)S(1)}, f32[8,72,512]{2,1,0:T(8,128)S(1)}, u32[]{:S(2)}, u32[]{:S(2)}) collective-permute-start(f32[8,72,512]{2,1,0:T(8,128)S(1)} %select_dynamic-update-slice_fusion.refs_3_), channel_id=1, source_target_pairs={{4,8},{8,4},{12,16},{16,12},{20,24},{24,20},{28,32},{32,28},{36,40... | collective-permute-start | bytes 3538952 | tf_op jit(solution)/shard_map/ppermute | solution.py:171
  73.9 2.5 %sweep.10.refs_0_ = f32[8,64,512]{2,1,0:T(8,128)S(1)} custom-call(s32[7,128]{1,0:T(8,128)S(1)} %concatenate.10.tag_ref, f32[192]{0:T(256)S(1)} %reshape.3.tab_ref, f32[8,80,512]{2,1,0:T(8,128)S(1)} %sweep.9.refs_0_, f32[8,80,512]{2,1,0:T(8,128)S(1)} %collective-permute-done.4.refs_1_, f32[8,80,512]{2,1,0:T(8,128)S(1)} %collective-permute-done.5.refs_2_), custom_call_target="tpu_custom_call" | custom-call | tf_op jit(solution)/shard_map/sweep/pallas_call | solution.py:154
  76.4 2.0 %collective-permute-start.7 = (f32[8,64,512]{2,1,0:T(8,128)S(1)}, f32[8,64,512]{2,1,0:T(8,128)S(1)}, u32[]{:S(2)}, u32[]{:S(2)}) collective-permute-start(f32[8,64,512]{2,1,0:T(8,128)S(1)} %sweep.10.refs_0_), channel_id=1, source_target_pairs={{4,8},{8,4},{12,16},{16,12},{20,24},{24,20},{28,32},{32,28},{36,40... | collective-permute-start | bytes 3145736 | tf_op jit(solution)/shard_map/ppermute | solution.py:171
  78.5 22.3 %collective-permute-done.7.refs_2_ = f32[8,64,512]{2,1,0:T(8,128)S(1)} collective-permute-done((f32[8,64,512]{2,1,0:T(8,128)S(1)}, f32[8,64,512]{2,1,0:T(8,128)S(1)}, u32[]{:S(2)}, u32[]{:S(2)}) %collective-permute-start.7) | collective-permute-done | bytes 1048608 | tf_op jit(solution)/shard_map/ppermute | solution.py:171
  100.8 4.0 %sweep.15.refs_3_ = f32[8,88,512]{2,1,0:T(8,128)S(1)} custom-call(s32[7,128]{1,0:T(8,128)S(1)} %concatenate.10.tag_ref, f32[192]{0:T(256)S(1)} %reshape.3.tab_ref, f32[8,64,512]{2,1,0:T(8,128)S(1)} %sweep.10.refs_0_, f32[8,64,512]{2,1,0:T(8,128)S(1)} %collective-permute-done.6.refs_1_, f32[8,64,512]{2,1,0:T(8,128)S(1)} %collective-permute-done.7.refs_2_, ...), custom_call_target="tpu_custom_call" | custom-call | tf_op jit(solution)/shard_map/sweep/pallas_call | solution.py:154
  104.8 3.4 %collective-permute-start.21 = (f32[8,88,512]{2,1,0:T(8,128)S(1)}, f32[8,88,512]{2,1,0:T(8,128)S(1)}, u32[]{:S(2)}, u32[]{:S(2)}) collective-permute-start(f32[8,88,512]{2,1,0:T(8,128)S(1)} %sweep.15.refs_3_), channel_id=1, source_target_pairs={{4,8},{8,4},{12,16},{16,12},{20,24},{24,20},{28,32},{32,28},{36,40... | collective-permute-start | bytes 4325384 | tf_op jit(solution)/shard_map/ppermute | solution.py:171
  108.2 2.2 %sweep.11.refs_0_ = f32[8,48,512]{2,1,0:T(8,128)S(1)} custom-call(s32[7,128]{1,0:T(8,128)S(1)} %concatenate.10.tag_ref, f32[192]{0:T(256)S(1)} %reshape.3.tab_ref, f32[8,64,512]{2,1,0:T(8,128)S(1)} %sweep.10.refs_0_, f32[8,64,512]{2,1,0:T(8,128)S(1)} %collective-permute-done.6.refs_1_, f32[8,64,512]{2,1,0:T(8,128)S(1)} %collective-permute-done.7.refs_2_), custom_call_target="tpu_custom_call" | custom-call | tf_op jit(solution)/shard_map/sweep/pallas_call | solution.py:154
  110.4 1.8 %collective-permute-start.9 = (f32[8,48,512]{2,1,0:T(8,128)S(1)}, f32[8,48,512]{2,1,0:T(8,128)S(1)}, u32[]{:S(2)}, u32[]{:S(2)}) collective-permute-start(f32[8,48,512]{2,1,0:T(8,128)S(1)} %sweep.11.refs_0_), channel_id=1, source_target_pairs={{4,8},{8,4},{12,16},{16,12},{20,24},{24,20},{28,32},{32,28},{36,40... | collective-permute-start | bytes 2359304 | tf_op jit(solution)/shard_map/ppermute | solution.py:171
  112.3 22.8 %collective-permute-done.9.refs_2_ = f32[8,48,512]{2,1,0:T(8,128)S(1)} collective-permute-done((f32[8,48,512]{2,1,0:T(8,128)S(1)}, f32[8,48,512]{2,1,0:T(8,128)S(1)}, u32[]{:S(2)}, u32[]{:S(2)}) %collective-permute-start.9) | collective-permute-done | bytes 786464 | tf_op jit(solution)/shard_map/ppermute | solution.py:171
  135.1 1.9 %sweep.16.refs_6_ = f32[8,32,512]{2,1,0:T(8,128)S(1)} custom-call(s32[7,128]{1,0:T(8,128)S(1)} %concatenate.10.tag_ref, f32[192]{0:T(256)S(1)} %reshape.3.tab_ref, f32[8,48,512]{2,1,0:T(8,128)S(1)} %sweep.11.refs_0_, f32[8,48,512]{2,1,0:T(8,128)S(1)} %collective-permute-done.8.refs_1_, f32[8,48,512]{2,1,0:T(8,128)S(1)} %collective-permute-done.9.refs_2_), custom_call_target="tpu_custom_call" | custom-call | tf_op jit(solution)/shard_map/sweep/pallas_call | solution.py:154
  137.0 4.8 %sweep.17 = f32[8,128,512]{2,1,0:T(8,128)} custom-call(s32[7,128]{1,0:T(8,128)S(1)} %concatenate.10.tag_ref, f32[192]{0:T(256)S(1)} %reshape.3.tab_ref, f32[8,48,512]{2,1,0:T(8,128)S(1)} %sweep.11.refs_0_, f32[8,48,512]{2,1,0:T(8,128)S(1)} %collective-permute-done.8.refs_1_, f32[8,48,512]{2,1,0:T(8,128)S(1)} %collective-permute-done.9.refs_2_, ...), custom_call_target="tpu_custom_call" | custom-call | tf_op jit(solution)/shard_map/sweep/pallas_call | solution.py:154
  (55 shorter events, 9.1 us)
Async XLA Ops:
  1.6 26.0 %collective-permute-start.3 = (f32[8,96,512]{2,1,0:T(8,128)S(1)}, f32[8,96,512]{2,1,0:T(8,128)S(1)}, u32[]{:S(2)}, u32[]{:S(2)}) collective-permute-start(f32[8,96,512]{2,1,0:T(8,128)S(1)} %slice.33.refs_0_), channel_id=1, source_target_pairs={{4,8},{8,4},{12,16},{16,12},{20,24},{24,20},{28,32},{32,28},{36,40... | collective-permute-start | bytes 4718600 | tf_op jit(solution)/shard_map/ppermute | solution.py:171
  9.4 18.2 %collective-permute-start.2 = (f32[8,96,512]{2,1,0:T(8,128)S(1)}, f32[8,96,512]{2,1,0:T(8,128)}, u32[]{:S(2)}, u32[]{:S(2)}) collective-permute-start(f32[8,96,512]{2,1,0:T(8,128)S(1)} %slice.33.refs_0_), channel_id=1, source_target_pairs={{0,4},{4,0},{8,12},{12,8},{16,20},{20,16},{24,28},{28,24},{32,36},... | collective-permute-start | bytes 4718600 | tf_op jit(solution)/shard_map/ppermute | solution.py:171
  10.4 8.4 %copy-start.1 = (s32[4,8,1,4]{1,3,2,0:T(4,128)S(1)}, s32[4,8,1,4]{1,3,2,0:T(4,128)}, u32[]{:S(2)}) copy-start(s32[4,8,1,4]{1,3,2,0:T(4,128)} %param.6) | copy-start | bytes 1540
  10.5 8.8 %copy-start.2 = (f32[16,3]{0,1:T(4,128)S(1)}, f32[16,3]{0,1:T(4,128)}, u32[]{:S(2)}) copy-start(f32[16,3]{0,1:T(4,128)} %param.7) | copy-start | bytes 580
  10.5 7.2 %collective-permute-start.11 = (f32[8,8,512]{2,1,0:T(8,128)S(1)}, f32[8,8,512]{2,1,0:T(8,128)S(1)}, u32[]{:S(2)}, u32[]{:S(2)}) collective-permute-start(f32[8,8,512]{2,1,0:T(8,128)S(1)} %get-tuple-element.7), channel_id=1, source_target_pairs={{1,2},{2,1},{3,0},{0,3},{5,6},{6,5},{7,4},{4,7},{9,10},{10,9},{11,... | collective-permute-start | bytes 393224 | tf_op jit(solution)/shard_map/ppermute | solution.py:171
  11.0 6.6 %collective-permute-start.10 = (f32[8,8,512]{2,1,0:T(8,128)S(1)}, f32[8,8,512]{2,1,0:T(8,128)S(1)}, u32[]{:S(2)}, u32[]{:S(2)}) collective-permute-start(f32[8,8,512]{2,1,0:T(8,128)S(1)} %get-tuple-element.8), channel_id=1, source_target_pairs={{0,1},{1,0},{2,3},{3,2},{4,5},{5,4},{6,7},{7,6},{8,9},{9,8},{10,11... | collective-permute-start | bytes 393224 | tf_op jit(solution)/shard_map/ppermute | solution.py:171
  18.7 18.0 %collective-permute-start.13 = (f32[8,40,512]{2,1,0:T(8,128)}, f32[8,40,512]{2,1,0:T(8,128)}, u32[]{:S(2)}, u32[]{:S(2)}) collective-permute-start(f32[8,40,512]{2,1,0:T(8,128)} %pad_maximum_fusion.refs_3_), channel_id=1, source_target_pairs={{4,8},{8,4},{12,16},{16,12},{20,24},{24,20},{28,32},{32,28},{36,40... | collective-permute-start | bytes 1966088 | tf_op jit(solution)/shard_map/ppermute | solution.py:171
  18.7 18.0 %collective-permute-start.12 = (f32[8,40,512]{2,1,0:T(8,128)}, f32[8,40,512]{2,1,0:T(8,128)}, u32[]{:S(2)}, u32[]{:S(2)}) collective-permute-start(f32[8,40,512]{2,1,0:T(8,128)} %pad_maximum_fusion.refs_3_), channel_id=1, source_target_pairs={{0,4},{4,0},{8,12},{12,8},{16,20},{20,16},{24,28},{28,24},{32,36},... | collective-permute-start | bytes 1966088 | tf_op jit(solution)/shard_map/ppermute | solution.py:171
  19.1 3.7 %collective-permute-start.1 = (s32[2,128]{1,0:T(2,128)S(1)}, s32[2,128]{1,0:T(2,128)S(1)}, u32[]{:S(2)}, u32[]{:S(2)}) collective-permute-start(s32[2,128]{1,0:T(2,128)S(1)} %pad_add_fusion), channel_id=1, source_target_pairs={{0,1},{1,0},{2,3},{3,2},{4,5},{5,4},{6,7},{7,6},{8,9},{9,8},{10,11... | collective-permute-start | bytes 3080 | tf_op jit(solution)/shard_map/ppermute | solution.py:171
  22.8 4.8 %collective-permute-start = (s32[2,128]{1,0:T(2,128)S(1)}, s32[2,128]{1,0:T(2,128)S(1)}, u32[]{:S(2)}, u32[]{:S(2)}) collective-permute-start(s32[2,128]{1,0:T(2,128)S(1)} %pad_add_fusion), channel_id=1, source_target_pairs={{1,2},{2,1},{3,0},{0,3},{5,6},{6,5},{7,4},{4,7},{9,10},{10,9},{11,... | collective-permute-start | bytes 3080 | tf_op jit(solution)/shard_map/ppermute | solution.py:171
  31.6 33.9 %collective-permute-start.5 = (f32[8,80,512]{2,1,0:T(8,128)S(1)}, f32[8,80,512]{2,1,0:T(8,128)S(1)}, u32[]{:S(2)}, u32[]{:S(2)}) collective-permute-start(f32[8,80,512]{2,1,0:T(8,128)S(1)} %sweep.9.refs_0_), channel_id=1, source_target_pairs={{4,8},{8,4},{12,16},{16,12},{20,24},{24,20},{28,32},{32,28},{36,40... | collective-permute-start | bytes 3932168 | tf_op jit(solution)/shard_map/ppermute | solution.py:171
  36.6 28.8 %collective-permute-start.4 = (f32[8,80,512]{2,1,0:T(8,128)S(1)}, f32[8,80,512]{2,1,0:T(8,128)S(1)}, u32[]{:S(2)}, u32[]{:S(2)}) collective-permute-start(f32[8,80,512]{2,1,0:T(8,128)S(1)} %sweep.9.refs_0_), channel_id=1, source_target_pairs={{0,4},{4,0},{8,12},{12,8},{16,20},{20,16},{24,28},{28,24},{32,36},... | collective-permute-start | bytes 3932168 | tf_op jit(solution)/shard_map/ppermute | solution.py:171
  41.1 20.7 %collective-permute-start.15 = (f32[8,56,512]{2,1,0:T(8,128)S(1)}, f32[8,56,512]{2,1,0:T(8,128)S(1)}, u32[]{:S(2)}, u32[]{:S(2)}) collective-permute-start(f32[8,56,512]{2,1,0:T(8,128)S(1)} %sweep.12.refs_3_.refs_0_), channel_id=1, source_target_pairs={{4,8},{8,4},{12,16},{16,12},{20,24},{24,20},{28,32},{32,28},{36,40... | collective-permute-start | bytes 2752520 | tf_op jit(solution)/shard_map/ppermute | solution.py:171
  44.3 17.5 %collective-permute-start.14 = (f32[8,56,512]{2,1,0:T(8,128)S(1)}, f32[8,56,512]{2,1,0:T(8,128)S(1)}, u32[]{:S(2)}, u32[]{:S(2)}) collective-permute-start(f32[8,56,512]{2,1,0:T(8,128)S(1)} %sweep.12.refs_3_.refs_0_), channel_id=1, source_target_pairs={{0,4},{4,0},{8,12},{12,8},{16,20},{20,16},{24,28},{28,24},{32,36},... | collective-permute-start | bytes 2752520 | tf_op jit(solution)/shard_map/ppermute | solution.py:171
  63.6 6.3 %collective-permute-start.17 = (f32[8,8,512]{2,1,0:T(8,128)S(1)}, f32[8,8,512]{2,1,0:T(8,128)S(1)}, u32[]{:S(2)}, u32[]{:S(2)}) collective-permute-start(f32[8,8,512]{2,1,0:T(8,128)S(1)} %get-tuple-element.9), channel_id=1, source_target_pairs={{1,2},{2,1},{3,0},{0,3},{5,6},{6,5},{7,4},{4,7},{9,10},{10,9},{11,... | collective-permute-start | bytes 393224 | tf_op jit(solution)/shard_map/ppermute | solution.py:171
  65.4 5.0 %collective-permute-start.16 = (f32[8,8,512]{2,1,0:T(8,128)S(1)}, f32[8,8,512]{2,1,0:T(8,128)S(1)}, u32[]{:S(2)}, u32[]{:S(2)}) collective-permute-start(f32[8,8,512]{2,1,0:T(8,128)S(1)} %get-tuple-element.10), channel_id=1, source_target_pairs={{0,1},{1,0},{2,3},{3,2},{4,5},{5,4},{6,7},{7,6},{8,9},{9,8},{10,11... | collective-permute-start | bytes 393224 | tf_op jit(solution)/shard_map/ppermute | solution.py:171
  70.5 30.3 %collective-permute-start.19 = (f32[8,72,512]{2,1,0:T(8,128)S(1)}, f32[8,72,512]{2,1,0:T(8,128)S(1)}, u32[]{:S(2)}, u32[]{:S(2)}) collective-permute-start(f32[8,72,512]{2,1,0:T(8,128)S(1)} %select_dynamic-update-slice_fusion.refs_3_), channel_id=1, source_target_pairs={{4,8},{8,4},{12,16},{16,12},{20,24},{24,20},{28,32},{32,28},{36,40... | collective-permute-start | bytes 3538952 | tf_op jit(solution)/shard_map/ppermute | solution.py:171
  73.9 26.9 %collective-permute-start.18 = (f32[8,72,512]{2,1,0:T(8,128)S(1)}, f32[8,72,512]{2,1,0:T(8,128)S(1)}, u32[]{:S(2)}, u32[]{:S(2)}) collective-permute-start(f32[8,72,512]{2,1,0:T(8,128)S(1)} %select_dynamic-update-slice_fusion.refs_3_), channel_id=1, source_target_pairs={{0,4},{4,0},{8,12},{12,8},{16,20},{20,16},{24,28},{28,24},{32,36},... | collective-permute-start | bytes 3538952 | tf_op jit(solution)/shard_map/ppermute | solution.py:171
  76.4 24.3 %collective-permute-start.7 = (f32[8,64,512]{2,1,0:T(8,128)S(1)}, f32[8,64,512]{2,1,0:T(8,128)S(1)}, u32[]{:S(2)}, u32[]{:S(2)}) collective-permute-start(f32[8,64,512]{2,1,0:T(8,128)S(1)} %sweep.10.refs_0_), channel_id=1, source_target_pairs={{4,8},{8,4},{12,16},{16,12},{20,24},{24,20},{28,32},{32,28},{36,40... | collective-permute-start | bytes 3145736 | tf_op jit(solution)/shard_map/ppermute | solution.py:171
  78.5 22.3 %collective-permute-start.6 = (f32[8,64,512]{2,1,0:T(8,128)S(1)}, f32[8,64,512]{2,1,0:T(8,128)S(1)}, u32[]{:S(2)}, u32[]{:S(2)}) collective-permute-start(f32[8,64,512]{2,1,0:T(8,128)S(1)} %sweep.10.refs_0_), channel_id=1, source_target_pairs={{0,4},{4,0},{8,12},{12,8},{16,20},{20,16},{24,28},{28,24},{32,36},... | collective-permute-start | bytes 3145736 | tf_op jit(solution)/shard_map/ppermute | solution.py:171
  104.8 32.2 %collective-permute-start.21 = (f32[8,88,512]{2,1,0:T(8,128)S(1)}, f32[8,88,512]{2,1,0:T(8,128)S(1)}, u32[]{:S(2)}, u32[]{:S(2)}) collective-permute-start(f32[8,88,512]{2,1,0:T(8,128)S(1)} %sweep.15.refs_3_), channel_id=1, source_target_pairs={{4,8},{8,4},{12,16},{16,12},{20,24},{24,20},{28,32},{32,28},{36,40... | collective-permute-start | bytes 4325384 | tf_op jit(solution)/shard_map/ppermute | solution.py:171
  108.2 28.8 %collective-permute-start.20 = (f32[8,88,512]{2,1,0:T(8,128)S(1)}, f32[8,88,512]{2,1,0:T(8,128)S(1)}, u32[]{:S(2)}, u32[]{:S(2)}) collective-permute-start(f32[8,88,512]{2,1,0:T(8,128)S(1)} %sweep.15.refs_3_), channel_id=1, source_target_pairs={{0,4},{4,0},{8,12},{12,8},{16,20},{20,16},{24,28},{28,24},{32,36},... | collective-permute-start | bytes 4325384 | tf_op jit(solution)/shard_map/ppermute | solution.py:171
  110.4 24.6 %collective-permute-start.9 = (f32[8,48,512]{2,1,0:T(8,128)S(1)}, f32[8,48,512]{2,1,0:T(8,128)S(1)}, u32[]{:S(2)}, u32[]{:S(2)}) collective-permute-start(f32[8,48,512]{2,1,0:T(8,128)S(1)} %sweep.11.refs_0_), channel_id=1, source_target_pairs={{4,8},{8,4},{12,16},{16,12},{20,24},{24,20},{28,32},{32,28},{36,40... | collective-permute-start | bytes 2359304 | tf_op jit(solution)/shard_map/ppermute | solution.py:171
  112.3 22.8 %collective-permute-start.8 = (f32[8,48,512]{2,1,0:T(8,128)S(1)}, f32[8,48,512]{2,1,0:T(8,128)S(1)}, u32[]{:S(2)}, u32[]{:S(2)}) collective-permute-start(f32[8,48,512]{2,1,0:T(8,128)S(1)} %sweep.11.refs_0_), channel_id=1, source_target_pairs={{0,4},{4,0},{8,12},{12,8},{16,20},{20,16},{24,28},{28,24},{32,36},... | collective-permute-start | bytes 2359304 | tf_op jit(solution)/shard_map/ppermute | solution.py:171
  (1 other events, 8.2 us)
